TPU v7x, 8 devices: a whole 2x2x1 slice. The times are simulated.
8 devices in a mesh: dp: 2 (over z, y), sp: 4 (over x, core).
Axes of the slice: x: 2, y: 2, z: 1, core: 2. Of those that a mesh axis runs over, the one named last changes fastest.
Arguments:
- x: bfloat16 [4, 4096], P('dp'), parts along dimension 0
- lens: int32 [4], P('dp'), parts along dimension 0
- wq: bfloat16 [2, 4096, 4096], replicated
- wk: bfloat16 [2, 4096, 4096], replicated
- wv: bfloat16 [2, 4096, 4096], replicated
- wo: bfloat16 [2, 4096, 4096], P(None, 'sp')
- w1: bfloat16 [2, 4096, 16384], P(None, None, 'sp')
- w2: bfloat16 [2, 16384, 4096], P(None, 'sp')
- g1: bfloat16 [2, 4096], replicated
- g2: bfloat16 [2, 4096], replicated
- kc: bfloat16 [2, 4, 2048, 32, 128], P(None, 'dp', 'sp'), parts along dimension 1
- vc: bfloat16 [2, 4, 2048, 32, 128], P(None, 'dp', 'sp'), parts along dimension 1
Outputs:
- output 1: bfloat16 [4, 4096], P('dp'), parts along dimension 0
- output 2: bfloat16 [2, 4, 2048, 32, 128], P(None, 'dp', 'sp'), parts along dimension 1
- output 3: bfloat16 [2, 4, 2048, 32, 128], P(None, 'dp', 'sp'), parts along dimension 1
There are 2 independent parts. A program takes and returns all parts, laid end to end along the dimension named above; an argument that names none is the same for every part.
All inputs are finite; a program needn't handle non-finite values.
Results may differ from a plain program's by a relative error of at most 0.00913119.
Values are sent between devices in bfloat16 or wider.
A program may use at most 1.75 GiB of HBM per device.

v0:
```python
import jax
import jax.numpy as jnp
from jax import lax
from jax.sharding import PartitionSpec as P

EPS = 1e-6


def _rms(h, g):
    r = lax.rsqrt(jnp.mean(h * h, axis=-1, keepdims=True) + EPS)
    return (h * r * g.astype(jnp.float32)).astype(jnp.bfloat16)


def _mm(a, w):
    return jnp.dot(a, w, preferred_element_type=jnp.float32)


def solution(mesh):
    sp = mesh.shape['sp']
    kspec = P(None, 'dp', 'sp', None, None)

    def local(x, lens, wq, wk, wv, wo, w1, w2, g1, g2, kc, vc):
        nl, b, s_dev, kvh, dh = kc.shape
        hq = wq.shape[-1] // dh
        grp = hq // kvh
        hl = hq // sp
        idx = lax.axis_index('sp')
        posn = idx * s_dev + jnp.arange(s_dev)
        write = (posn[None, :] == (lens - 1)[:, None])[:, :, None, None]
        valid = (posn[None, :] < lens[:, None])[:, None, None, :]
        h = x.astype(jnp.float32)
        ks, vs = [], []
        for l in range(nl):
            xn = _rms(h, g1[l])
            q = _mm(xn, wq[l]).astype(jnp.bfloat16).reshape(b, kvh, grp, dh)
            k = _mm(xn, wk[l]).astype(jnp.bfloat16).reshape(b, 1, kvh, dh)
            v = _mm(xn, wv[l]).astype(jnp.bfloat16).reshape(b, 1, kvh, dh)
            kl = jnp.where(write, k, kc[l])
            vl = jnp.where(write, v, vc[l])
            ks.append(kl)
            vs.append(vl)
            s = jnp.einsum('bkgd,bskd->bkgs', q, kl, preferred_element_type=jnp.float32) * dh ** -0.5
            s = jnp.where(valid, s, -jnp.inf)
            m = jnp.max(s, axis=-1)
            p = jnp.exp(s - jnp.where(jnp.isfinite(m), m, 0.0)[..., None])
            den = jnp.sum(p, axis=-1)
            o = jnp.einsum('bkgs,bskd->bkgd', p.astype(jnp.bfloat16), vl, preferred_element_type=jnp.float32)
            c = jnp.exp(m - lax.pmax(m, 'sp'))
            o, den = lax.psum((o * c[..., None], den * c), 'sp')
            att = (o / den[..., None]).astype(jnp.bfloat16).reshape(b, hq, dh)
            att = lax.dynamic_slice_in_dim(att, idx * hl, hl, axis=1).reshape(b, hl * dh)
            h = h + lax.psum(_mm(att, wo[l]), 'sp')
            u = jax.nn.gelu(_mm(_rms(h, g2[l]), w1[l])).astype(jnp.bfloat16)
            h = h + lax.psum(_mm(u, w2[l]), 'sp')
        return h.astype(jnp.bfloat16), jnp.stack(ks), jnp.stack(vs)

    return jax.shard_map(
        local, mesh=mesh,
        in_specs=(P('dp', None), P('dp'), P(), P(), P(), P(None, 'sp', None), P(None, None, 'sp'),
                  P(None, 'sp', None), P(), P(), kspec, kspec),
        out_specs=(P('dp', None), kspec, kspec), check_vma=False)
```

profile of v0, /device:TPU:0, one launch (start us, length us, event | category | flops | bytes accessed | tf_op | source)
XLA Modules:
  0.0 316.7 jit_solution(4374463664164806723)
XLA Ops:
  0.6 0.7 broadcast_add_fusion
  1.3 0.9 fusion.86
  2.2 0.7 broadcast_compare_fusion.1
  2.9 0.8 slice_convert_fusion.1
  3.7 0.0 copy-start
  3.7 14.9 %fusion.71 = bf16[1,2,32,128]{3,1,2,0:T(2,128)(2,1)S(1)} fusion(bf16[2,4096,4096]{2,1,0:T(8,128)(2,1)} %param.15, bf16[2,4096]{1,0:T(2,128)(2,1)} %param.12, f32[2]{0:T(128)S(1)} %add_rsqrt_fusion.3, f32[4096]{0:T(1024)S(1)} %bitcast.175), kind=kOutput, calls=%fused_computation.63 | convolution fusion | flops 67149824 | bytes 33603592 | tf_op jit(solution)/shard_map/dot_general | solution.py:15
  18.6 0.0 copy-done
  18.6 12.9 %fusion.68 = bf16[1,2,32,128]{3,1,2,0:T(2,128)(2,1)S(1)} fusion(bf16[2,4096,4096]{2,1,0:T(8,128)(2,1)} %param.16, bf16[2,4096]{1,0:T(2,128)(2,1)S(1)} %copy-done, f32[2]{0:T(128)S(1)} %add_rsqrt_fusion.3, f32[4096]{0:T(1024)S(1)} %bitcast.176), kind=kOutput, calls=%fused_computation.62 | convolution fusion | flops 67149824 | bytes 33603592 | tf_op jit(solution)/shard_map/dot_general | solution.py:15
  31.5 0.0 copy-start.1
  31.5 12.9 %fusion.44 = bf16[2,4096]{1,0:T(2,128)(2,1)S(1)} fusion(bf16[2,4096,4096]{2,1,0:T(8,128)(2,1)} %param.14, bf16[2,4096]{1,0:T(2,128)(2,1)S(1)} %copy-done, f32[2]{0:T(128)S(1)} %add_rsqrt_fusion.3, f32[4096]{0:T(1024)S(1)} %bitcast.177), kind=kOutput, calls=%fused_computation.54 | convolution fusion | flops 67149824 | bytes 33603592 | tf_op jit(solution)/shard_map/dot_general | solution.py:15
  44.4 0.0 copy-done.1
  44.5 9.4 %bitcast_select_fusion.2 = (bf16[2,512,32,128]{3,2,1,0:T(8,128)(2,1)}, bf16[2,512,32,128]{3,2,1,0:T(8,128)(2,1)S(1)}) fusion(pred[2,512]{1,0:T(4,128)(4,1)S(1)} %get-tuple-element.34, bf16[2,2,512,32,128]{4,3,2,1,0:T(8,128)(2,1)} %param.23, bf16[2,32,128]{2,1,0:T(8,128)(2,1)S(1)} %get-tuple-element.35, bf16[2,2,512,32,128]{4,3,2,1,0:T(8,128)(2,1)} %param.22, ...), kind=kLoop, calls=%fused_computation.38 | loop fusion | flops 8388608 | bytes 33588224 | tf_op jit(solution)/shard_map/jit(_where)/select_n | solution.py:39
  53.9 8.3 %fusion.40 = f32[2,32,1,512]{3,2,1,0:T(1,128)S(1)} fusion(bf16[2,32,128,1]{2,3,1,0:T(2,128)(2,1)S(1)} %reshape.200, bf16[2,512,32,128]{3,2,1,0:T(8,128)(2,1)S(1)} %get-tuple-element.32), kind=kOutput, calls=%fused_computation.46 | convolution fusion | flops 8388608 | bytes 8536064 | tf_op jit(solution)/shard_map/bkgd,bskd->bkgs/dot_general | solution.py:42
  62.2 0.1 fusion.82
  62.3 9.1 %pmax.14 = f32[2,32,1]{1,0,2:T(2,128)S(1)} all-reduce(f32[2,32,1]{1,0,2:T(2,128)S(1)} %bitcast.187), channel_id=1, replica_groups=mesh['dp'=2,'sp'=4] {'sp'}, use_global_device_ids=true, to_apply=%region_2.3 | all-reduce | flops 64 | bytes 512 | tf_op jit(solution)/shard_map/pmax | solution.py:48
  71.4 0.2 fusion.85
  71.6 11.7 %fusion.38 = f32[2,32,1,128]{3,2,1,0:T(1,128)S(1)} fusion(bf16[2,512,32,128]{3,2,1,0:T(8,128)(2,1)} %get-tuple-element.31, bf16[2,32,512,1]{2,1,0,3:T(8,128)(2,1)S(1)} %get-tuple-element.17), kind=kOutput, calls=%fused_computation.44 | convolution fusion | flops 8388608 | bytes 8486912 | tf_op jit(solution)/shard_map/bkgs,bskd->bkgd/dot_general | solution.py:47
  83.3 0.1 multiply_bitcast_fusion.1
  83.4 10.5 %all-reduce.1 = (f32[2,32]{1,0:T(2,128)S(1)}, f32[2,32,1,128]{3,1,0,2:T(8,128)S(1)}) all-reduce(f32[2,32]{1,0:T(2,128)S(1)} %get-tuple-element.30, f32[2,32,1,128]{3,1,0,2:T(8,128)S(1)} %multiply_bitcast_fusion.1), channel_id=1, replica_groups=mesh['dp'=2,'sp'=4] {'sp'}, use_global_device_ids=true, to_apply=%region_5.6 | all-reduce | flops 8256 | bytes 66048 | tf_op jit(solution)/shard_map/psum | solution.py:49
  93.9 0.1 constant_dynamic-slice_fusion.1
  94.0 0.1 fusion.135
  94.1 4.6 %fusion.32 = f32[2,4096]{1,0:T(2,128)S(1)} fusion(bf16[2,1024,4096]{2,1,0:T(8,128)(2,1)} %param.17, bf16[1,2,8,128]{3,2,1,0:T(8,128)(2,1)S(1)} %fusion.135), kind=kOutput, calls=%fused_computation.36 | convolution fusion | flops 16777216 | bytes 8425472 | tf_op jit(solution)/shard_map/dot_general | solution.py:15
  98.7 10.5 %psum.58 = f32[2,4096]{1,0:T(2,128)S(1)} all-reduce(f32[2,4096]{1,0:T(2,128)S(1)} %fusion.32), channel_id=1, replica_groups=mesh['dp'=2,'sp'=4] {'sp'}, use_global_device_ids=true, to_apply=%region_6.7 | all-reduce | flops 8192 | bytes 65536 | tf_op jit(solution)/shard_map/psum | solution.py:52
  109.2 0.1 multiply_reduce_fusion.2
  109.3 22.7 %fusion.10 = f32[2,4096]{1,0:T(2,128)S(1)} fusion(bf16[2,4096,4096]{2,1,0:T(8,128)(2,1)} %param.19, bf16[2,4096,4096]{2,1,0:T(8,128)(2,1)} %param.18, f32[2]{0:T(128)S(1)} %add_rsqrt_fusion.2, f32[4096]{0:T(1024)S(1)} %bitcast.178, f32[2,4096]{1,0:T(2,128)S(1)} %psum.58, bf16[2,4096]{1,0:T(2,128)(2,1)S(1)} %copy-done), kind=kOutput, calls=%fused_computation.10 | convolution fusion | flops 134332416 | bytes 67207176 | tf_op jit(solution)/shard_map/dot_general | solution.py:15
  132.1 10.3 %psum.59 = f32[2,4096]{1,0:T(2,128)S(1)} all-reduce(f32[2,4096]{1,0:T(2,128)S(1)} %fusion.10), channel_id=1, replica_groups=mesh['dp'=2,'sp'=4] {'sp'}, use_global_device_ids=true, to_apply=%region_8.9 | all-reduce | flops 8192 | bytes 65536 | tf_op jit(solution)/shard_map/psum | solution.py:54
  142.3 0.2 multiply_reduce_fusion.1
  142.5 12.9 %fusion.65 = bf16[1,2,32,128]{3,1,2,0:T(2,128)(2,1)S(1)} fusion(bf16[2,4096,4096]{2,1,0:T(8,128)(2,1)} %param.15, f32[2,4096]{1,0:T(2,128)S(1)} %get-tuple-element.10, f32[2]{0:T(128)S(1)} %add_rsqrt_fusion.1, f32[4096]{0:T(1024)S(1)} %bitcast.172), kind=kOutput, calls=%fused_computation.61 | convolution fusion | flops 67141632 | bytes 33619976 | tf_op jit(solution)/shard_map/dot_general | solution.py:15
  155.4 12.9 %fusion.62 = bf16[1,2,32,128]{3,1,2,0:T(2,128)(2,1)S(1)} fusion(bf16[2,4096,4096]{2,1,0:T(8,128)(2,1)} %param.16, f32[2,4096]{1,0:T(2,128)S(1)} %get-tuple-element.10, f32[2]{0:T(128)S(1)} %add_rsqrt_fusion.1, f32[4096]{0:T(1024)S(1)} %bitcast.173), kind=kOutput, calls=%fused_computation.60 | convolution fusion | flops 67141632 | bytes 33619976 | tf_op jit(solution)/shard_map/dot_general | solution.py:15
  168.2 12.9 %fusion.53 = bf16[2,4096]{1,0:T(2,128)(2,1)S(1)} fusion(bf16[2,4096,4096]{2,1,0:T(8,128)(2,1)} %param.14, f32[2,4096]{1,0:T(2,128)S(1)} %get-tuple-element.10, f32[2]{0:T(128)S(1)} %add_rsqrt_fusion.1, f32[4096]{0:T(1024)S(1)} %bitcast.174), kind=kOutput, calls=%fused_computation.57 | convolution fusion | flops 67141632 | bytes 33619976 | tf_op jit(solution)/shard_map/dot_general | solution.py:15
  181.1 9.4 %bitcast_select_fusion = (bf16[2,512,32,128]{3,2,1,0:T(8,128)(2,1)}, bf16[2,512,32,128]{3,2,1,0:T(8,128)(2,1)S(1)}) fusion(pred[2,512]{1,0:T(4,128)(4,1)S(1)} %get-tuple-element.34, bf16[2,2,512,32,128]{4,3,2,1,0:T(8,128)(2,1)} %param.23, bf16[2,32,128]{2,1,0:T(8,128)(2,1)S(1)} %bitcast.182, bf16[2,2,512,32,128]{4,3,2,1,0:T(8,128)(2,1)} %param.22, ...), kind=kLoop, calls=%fused_computation.34 | loop fusion | flops 8388608 | bytes 33588224 | tf_op jit(solution)/shard_map/jit(_where)/select_n | solution.py:39
  190.6 8.3 %fusion.36 = f32[2,32,1,512]{3,2,1,0:T(1,128)S(1)} fusion(bf16[2,32,128,1]{2,3,1,0:T(2,128)(2,1)S(1)} %reshape.202, bf16[2,512,32,128]{3,2,1,0:T(8,128)(2,1)S(1)} %get-tuple-element.28), kind=kOutput, calls=%fused_computation.42 | convolution fusion | flops 8388608 | bytes 8536064 | tf_op jit(solution)/shard_map/bkgd,bskd->bkgs/dot_general | solution.py:42
  198.9 0.1 fusion.83
  199.0 6.4 %pmax.15 = f32[2,32,1]{1,0,2:T(2,128)S(1)} all-reduce(f32[2,32,1]{1,0,2:T(2,128)S(1)} %bitcast.186), channel_id=1, replica_groups=mesh['dp'=2,'sp'=4] {'sp'}, use_global_device_ids=true, to_apply=%region_11.12 | all-reduce | flops 64 | bytes 512 | tf_op jit(solution)/shard_map/pmax | solution.py:48
  205.4 0.2 fusion.84
  205.6 11.7 %fusion.34 = f32[2,32,1,128]{3,2,1,0:T(1,128)S(1)} fusion(bf16[2,512,32,128]{3,2,1,0:T(8,128)(2,1)} %get-tuple-element.27, bf16[2,32,512,1]{2,1,0,3:T(8,128)(2,1)S(1)} %get-tuple-element.15), kind=kOutput, calls=%fused_computation.40 | convolution fusion | flops 8388608 | bytes 8486912 | tf_op jit(solution)/shard_map/bkgs,bskd->bkgd/dot_general | solution.py:47
  217.3 0.1 multiply_bitcast_fusion
  217.4 11.0 %all-reduce = (f32[2,32]{1,0:T(2,128)S(1)}, f32[2,32,1,128]{3,1,0,2:T(8,128)S(1)}) all-reduce(f32[2,32]{1,0:T(2,128)S(1)} %get-tuple-element.26, f32[2,32,1,128]{3,1,0,2:T(8,128)S(1)} %multiply_bitcast_fusion), channel_id=1, replica_groups=mesh['dp'=2,'sp'=4] {'sp'}, use_global_device_ids=true, to_apply=%region_14.15 | all-reduce | flops 8256 | bytes 66048 | tf_op jit(solution)/shard_map/psum | solution.py:49
  228.4 0.1 constant_dynamic-slice_fusion
  228.5 0.1 fusion.136
  228.6 4.6 %fusion.30 = f32[2,4096]{1,0:T(2,128)S(1)} fusion(bf16[2,1024,4096]{2,1,0:T(8,128)(2,1)} %param.17, bf16[1,2,8,128]{3,2,1,0:T(8,128)(2,1)S(1)} %fusion.136), kind=kOutput, calls=%fused_computation.32 | convolution fusion | flops 16777216 | bytes 8425472 | tf_op jit(solution)/shard_map/dot_general | solution.py:15
  233.1 10.6 %psum.62 = f32[2,4096]{1,0:T(2,128)S(1)} all-reduce(f32[2,4096]{1,0:T(2,128)S(1)} %fusion.30), channel_id=1, replica_groups=mesh['dp'=2,'sp'=4] {'sp'}, use_global_device_ids=true, to_apply=%region_15.16 | all-reduce | flops 8192 | bytes 65536 | tf_op jit(solution)/shard_map/psum | solution.py:52
  243.8 0.1 multiply_reduce_fusion
  243.9 22.7 %fusion = f32[2,4096]{1,0:T(2,128)S(1)} fusion(bf16[2,4096,4096]{2,1,0:T(8,128)(2,1)} %param.19, bf16[2,4096,4096]{2,1,0:T(8,128)(2,1)} %param.18, f32[2,4096]{1,0:T(2,128)S(1)} %get-tuple-element.8, f32[2]{0:T(128)S(1)} %add_rsqrt_fusion, f32[4096]{0:T(1024)S(1)} %bitcast.179), kind=kOutput, calls=%fused_computation | convolution fusion | flops 134316032 | bytes 67190792 | tf_op jit(solution)/shard_map/dot_general | solution.py:15
  266.7 10.5 %psum.63 = f32[2,4096]{1,0:T(2,128)S(1)} all-reduce(f32[2,4096]{1,0:T(2,128)S(1)} %fusion), channel_id=1, replica_groups=mesh['dp'=2,'sp'=4] {'sp'}, use_global_device_ids=true, to_apply=%region_17.18 | all-reduce | flops 8192 | bytes 65536 | tf_op jit(solution)/shard_map/psum | solution.py:54
  277.2 0.6 add_convert_fusion
  277.8 17.8 %broadcast_select_fusion.1 = (bf16[1,2,512,32,128]{4,3,2,1,0:T(8,128)(2,1)}, bf16[1,2,512,32,128]{4,3,2,1,0:T(8,128)(2,1)}, bf16[1,2,512,32,128]{4,3,2,1,0:T(8,128)(2,1)S(1)}, bf16[1,2,512,32,128]{4,3,2,1,0:T(8,128)(2,1)S(1)}) fusion(pred[2,512]{1,0:T(4,128)(4,1)S(1)} %get-tuple-element.34, bf16[2,2,512,32,128]{4,3,2,1,0:T(8,128)(2,1)} %param.23, ...), kind=kLoop, calls=%fused_computation.51 | loop fusion | flops 16777216 | bytes 67175424 | tf_op jit(solution)/shard_map/jit(_where)/select_n | solution.py:39
  295.6 13.8 %pad_maximum_fusion.1 = bf16[2,2,512,32,128]{4,3,2,1,0:T(8,128)(2,1)} fusion(bf16[1,2,512,32,128]{4,3,2,1,0:T(8,128)(2,1)} %get-tuple-element.12, bf16[1,2,512,32,128]{4,3,2,1,0:T(8,128)(2,1)} %get-tuple-element.11), kind=kLoop, calls=%fused_computation.31 | loop fusion | flops 8388608 | bytes 33554432 | tf_op jit(solution)/shard_map/stack | solution.py:55
  309.4 6.7 %pad_maximum_fusion = bf16[2,2,512,32,128]{4,3,2,1,0:T(8,128)(2,1)} fusion(bf16[1,2,512,32,128]{4,3,2,1,0:T(8,128)(2,1)S(1)} %get-tuple-element.23, bf16[1,2,512,32,128]{4,3,2,1,0:T(8,128)(2,1)S(1)} %get-tuple-element.24), kind=kLoop, calls=%fused_computation.30 | loop fusion | flops 8388608 | bytes 33554432 | tf_op jit(solution)/shard_map/stack | solution.py:55
  (15 shorter events, 0.1 us)
Async XLA Ops:
  3.7 14.9 %copy-start = (bf16[2,4096]{1,0:T(2,128)(2,1)S(1)}, bf16[2,4096]{1,0:T(2,128)(2,1)}, u32[]{:S(2)}) copy-start(bf16[2,4096]{1,0:T(2,128)(2,1)} %param.12) | copy-start | bytes 49156
  31.5 12.9 %copy-start.1 = (bf16[2,4096]{1,0:T(2,128)(2,1)S(1)}, bf16[2,4096]{1,0:T(2,128)(2,1)}, u32[]{:S(2)}) copy-start(bf16[2,4096]{1,0:T(2,128)(2,1)} %param.21) | copy-start | bytes 49156
where the time goes:
time: 323 us; the launch traced here: 317 us
  matrix products  174 us (54%)
  blocking collectives  78.9 us (24%)
  other arithmetic  62.3 us (19%)
    dot_general x10, matrix products, _mm(): return jnp.dot(a, w, preferred_element_type=jnp.float32)  134 us
    select_n x3, other arithmetic, local(): vl = jnp.where(write, v, vc[l])  36.7 us
    dot_general x2, matrix products, local(): jnp.einsum('bkgs,bskd->bkgd', p.astype(jnp.bfloat16), vl, preferred_eleme...  23.4 us
    psum x2, blocking collectives, local(): o, den = lax.psum((o * c[..., None], den * c), 'sp')  21.5 us
    psum x2, blocking collectives, local(): h = h + lax.psum(_mm(att, wo[l]), 'sp')  21.1 us
    psum x2, blocking collectives, local(): h = h + lax.psum(_mm(u, w2[l]), 'sp')  20.8 us
    another operation x2, other arithmetic, local(): return (h.astype(jnp.bfloat16), jnp.stack(ks), jnp.stack(vs))  20.5 us
    dot_general x2, matrix products, local(): jnp.einsum('bkgd,bskd->bkgs', q, kl, preferred_element_type=jnp.float32)  16.6 us

commit v1 on v0

v1 whole, which is shorter than its diff:
```python
import functools

import jax
import jax.numpy as jnp
from jax import lax
from jax.experimental import pallas as pl
from jax.experimental.pallas import tpu as pltpu
from jax.sharding import PartitionSpec as P

EPS = 1e-6
MESH = pl.DeviceIdType.MESH
VM = pl.BlockSpec(memory_space=pltpu.VMEM)
ANY = pl.BlockSpec(memory_space=pl.ANY)
SM = pl.BlockSpec(memory_space=pltpu.SMEM)
F32, BF16 = jnp.float32, jnp.bfloat16
CH = 128
NB = 512


def _rms(h, g):
    r = lax.rsqrt(jnp.mean(h * h, axis=-1, keepdims=True) + EPS)
    return (h * r * g.astype(F32)).astype(BF16)


def _gelu(z):
    return 0.5 * z * (1.0 + jnp.tanh(0.7978845608028654 * (z + 0.044715 * z * z * z)))


def _dot(a, w):
    return jnp.dot(a, w, preferred_element_type=F32)


def _ids():
    dp, sp = lax.axis_index('dp'), lax.axis_index('sp')
    return dp, sp, lax.rem(sp, 2), dp * 4 + sp


def _barrier(me):
    sem = pltpu.get_barrier_semaphore()
    for k in range(1, 8):
        d = lax.rem(me + k, 8)
        pl.semaphore_signal(sem, inc=1, device_id=(d // 4, lax.rem(d, 4)), device_id_type=MESH)
    pl.semaphore_wait(sem, 7)


def _exchange(me, src, dst, ssem, rsem):
    out = []
    for k in range(1, 8):
        d = lax.rem(me + k, 8)
        c = pltpu.make_async_remote_copy(src(d), dst, ssem.at[k], rsem.at[k],
                                         device_id=(d // 4, lax.rem(d, 4)), device_id_type=MESH)
        c.start()
        out.append(c)
    return out


def _qkv_copies(l, me, ws, wbuf, wsem, slot, s0):
    out = []
    for i in range(3):
        for kh in range(2):
            n = 2 * i + kh
            out.append(pltpu.make_async_copy(
                ws[i].at[l, pl.ds(kh * 2048, 2048), pl.ds(pl.multiple_of(me * NB, NB), NB)],
                wbuf.at[slot + n], wsem.at[s0 + n]))
    return out


def _half_cols(t, q, c):
    half = (1 - c) if t < 2 else c
    return half * 2048 + q * 1024 + (t % 2) * NB


def _mlp_copies(l, dp, c, wo, w1, w2, wbuf, wsem):
    out = []
    for t in range(4):
        for q in range(2):
            n = 2 * t + q
            col = pl.multiple_of(_half_cols(t, q, c), NB)
            out.append(pltpu.make_async_copy(
                wo.at[l, pl.ds(pl.multiple_of(dp * 512, 512), 512), pl.ds(col, NB)],
                wbuf.at[n // 4, pl.ds((n % 4) * 512, 512)], wsem.at[n]))
    for j in range(4):
        for kh in range(2):
            n = 2 * j + kh
            out.append(pltpu.make_async_copy(
                w1.at[l, pl.ds(kh * 2048, 2048), pl.ds(pl.multiple_of(dp * 2048 + j * NB, NB), NB)],
                wbuf.at[2 + n], wsem.at[8 + n]))
    for t in range(4):
        for q in range(2):
            n = 2 * t + q
            col = pl.multiple_of(_half_cols(t, q, c), NB)
            out.append(pltpu.make_async_copy(
                w2.at[l, pl.ds(pl.multiple_of(dp * 2048, 2048), 2048), pl.ds(col, NB)],
                wbuf.at[10 + n], wsem.at[16 + n]))
    return out


def _allreduce(block, dp, sp, c, me, buf, sems, h_ref):
    psend, pown, precv, chips, tot = buf
    s1, r1, s2, r2, s3, r3 = sems
    partner = (dp, sp + 1 - 2 * c)
    for t in range(2):
        v = jnp.concatenate([block(t, 0)[0:4], block(t, 1)[0:4]], axis=0)
        psend[:, t * NB:(t + 1) * NB] = v
    one = pltpu.make_async_remote_copy(psend, precv, s1, r1, device_id=partner, device_id_type=MESH)
    one.start()
    for t in range(2):
        v = jnp.concatenate([block(t + 2, 0)[0:4], block(t + 2, 1)[0:4]], axis=0)
        pown[:, t * NB:(t + 1) * NB] = v
    one.wait()
    chip = dp * 2 + sp // 2
    chips[chip] = pown[...] + precv[...]
    two = []
    for k in range(1, 4):
        d = lax.rem(chip + k, 4)
        cp = pltpu.make_async_remote_copy(chips.at[chip], chips.at[chip], s2.at[k], r2.at[k],
                                          device_id=(d // 2, lax.rem(d, 2) * 2 + c), device_id_type=MESH)
        cp.start()
        two.append(cp)
    for cp in two:
        cp.wait()
    tot[c] = ((chips[0] + chips[1]) + chips[2]) + chips[3]
    three = pltpu.make_async_remote_copy(tot.at[c], tot.at[c], s3, r3, device_id=partner, device_id_type=MESH)
    three.start()
    three.wait()
    for half in range(2):
        for q in range(2):
            lo = half * 2048 + q * 1024
            h_ref[0:4, lo:lo + 1024] += tot[half, q * 4:q * 4 + 4, :]


def _qkv_stage(me, xn, wbuf, copies, slot, sendA, recvA, ssem, rsem, qkv_ref):
    res = []
    for i in range(3):
        copies[2 * i].wait()
        z = _dot(xn[:, :2048], wbuf[slot + 2 * i])
        copies[2 * i + 1].wait()
        z = z + _dot(xn[:, 2048:], wbuf[slot + 2 * i + 1])
        res.append(z)
    for g in range(2):
        rows = [r[2 * g:2 * g + 2] for r in res] + [jnp.zeros((2, NB), F32)]
        sendA[g] = jnp.concatenate(rows, axis=0).astype(BF16)
    cps = _exchange(me, lambda d: sendA.at[d // 4], recvA.at[me], ssem, rsem)
    recvA[me] = sendA[me // 4]
    for cp in cps:
        cp.wait()
    qkv_ref[...] = recvA[...]


def _first(x_ref, wq, wk, wv, g1, h_ref, qkv_ref, wbuf, xo, sendA, recvA, wsem, xs, xr, sa, ra):
    dp, sp, c, me = _ids()
    cq = _qkv_copies(0, me, (wq, wk, wv), wbuf, wsem, 0, 0)
    for cp in cq:
        cp.start()
    _barrier(me)
    ex = pltpu.make_async_remote_copy(x_ref, xo, xs, xr, device_id=(1 - dp, sp), device_id_type=MESH)
    ex.start()
    ex.wait()
    mine, other = x_ref[...].astype(F32), xo[...].astype(F32)
    h_ref[0:2, :] = jnp.where(dp == 0, mine, other)
    h_ref[2:4, :] = jnp.where(dp == 0, other, mine)
    h_ref[4:8, :] = jnp.zeros((4, h_ref.shape[1]), F32)
    xn = _rms(h_ref[...], g1[0:1, :])
    _qkv_stage(me, xn, wbuf, cq, 0, sendA, recvA, sa, ra, qkv_ref)


def _layer(l, last, *refs):
    if last:
        (op_ref, hin, wo, w1, w2, g2, y_ref, h_ref, *sc) = refs
    else:
        (op_ref, hin, wo, w1, w2, g2, wq, wk, wv, g1, h_ref, qkv_ref, *sc) = refs
    wbuf, recvB, att, u, psend, pown, precv, chips, tot = sc[:9]
    wsem, sb, rb, s1, r1, s2, r2, s3, r3 = sc[9:18]
    dp, sp, c, me = _ids()
    cm = _mlp_copies(l, dp, c, wo, w1, w2, wbuf, wsem)
    cq = []
    if not last:
        sendA, recvA, sa, ra = sc[18:]
        cq = _qkv_copies(l + 1, me, (wq, wk, wv), wbuf, wsem, 18, 24)
    for cp in cm + cq:
        cp.start()
    _barrier(me)
    cps = _exchange(me, lambda d: op_ref.at[2 * lax.rem(d, 4) + d // 4], recvB.at[me], sb, rb)
    recvB[me] = op_ref[2 * sp + dp]
    h_ref[...] = hin[...]
    att[...] = jnp.zeros_like(att)
    for cp in cps:
        cp.wait()
    for g in range(2):
        ms = [recvB[4 * g + i, 1][:, 0:1] for i in range(4)]
        m = functools.reduce(jnp.maximum, ms)
        o = jnp.zeros((8, 128), F32)
        den = jnp.zeros((8, 1), F32)
        for i in range(4):
            e = jnp.exp(ms[i] - m)
            o = o + recvB[4 * g + i, 0] * e
            den = den + recvB[4 * g + i, 1][:, 64:65] * e
        a = o / den
        for b in range(2):
            for j in range(4):
                att[2 * g + b:2 * g + b + 1, j * 128:(j + 1) * 128] = a[4 * b + j:4 * b + j + 1]
    av = att[...].astype(BF16)

    def wo_block(t, q):
        n = 2 * t + q
        cm[n].wait()
        return _dot(av, wbuf[n // 4, (n % 4) * 512:(n % 4) * 512 + 512, :])

    def bufs(i):
        return [psend.at[i], pown.at[i], precv.at[i], chips.at[i], tot.at[i]]

    def sems(i):
        return [s1.at[i], r1.at[i], s2.at[i], r2.at[i], s3.at[i], r3.at[i]]

    _allreduce(wo_block, dp, sp, c, me, bufs(0), sems(0), h_ref)
    xn = _rms(h_ref[...], g2[l:l + 1, :])
    for j in range(4):
        cm[8 + 2 * j].wait()
        z = _dot(xn[:, :2048], wbuf[2 + 2 * j])
        cm[9 + 2 * j].wait()
        z = z + _dot(xn[:, 2048:], wbuf[3 + 2 * j])
        u[:, j * NB:(j + 1) * NB] = _gelu(z).astype(BF16)
    uv = u[...]

    def w2_block(t, q):
        n = 2 * t + q
        cm[16 + n].wait()
        return _dot(uv, wbuf[10 + n])

    _allreduce(w2_block, dp, sp, c, me, bufs(1), sems(1), h_ref)
    if last:
        hv = h_ref[...]
        y_ref[...] = jnp.where(dp == 0, hv[0:2], hv[2:4]).astype(BF16)
    else:
        xn = _rms(h_ref[...], g1[l + 1:l + 2, :])
        _qkv_stage(me, xn, wbuf, cq, 18, sendA, recvA, sa, ra, qkv_ref)


def _attn(l, *refs):
    if l == 0:
        lens, qkv, kc, vc, ko, vo, op_ref, *sc = refs
    else:
        lens, qkv, kc, vc, _, _, ko, vo, op_ref, *sc = refs
    kb, vb, tr, s_ref, m_ref, l_ref, o_ref, ki, vi, kos, vos = sc
    nb, npos, nh, dh = kb.shape
    per = npos // CH
    n = nb * per
    base = lax.axis_index('sp') * npos

    def rd(src, buf, sem, i):
        b, p = i // per, pl.multiple_of(lax.rem(i, per) * CH, CH)
        return pltpu.make_async_copy(src.at[l, b, pl.ds(p, CH)], buf.at[b, pl.ds(p, CH)], sem.at[i])

    def wr(dst, buf, sem, i):
        b, p = i // per, pl.multiple_of(lax.rem(i, per) * CH, CH)
        return pltpu.make_async_copy(buf.at[b, pl.ds(p, CH)], dst.at[l, b, pl.ds(p, CH)], sem.at[i])

    for i in range(n):
        rd(kc, kb, ki, i).start()
    for i in range(n):
        rd(vc, vb, vi, i).start()
    for src in range(8):
        v = qkv[src].astype(F32)
        for j in range(4):
            tr[src * 4 + j] = v[:, j * dh:(j + 1) * dh]
    m_ref[...] = jnp.full(m_ref.shape, -jnp.inf, F32)
    l_ref[...] = jnp.zeros_like(l_ref)
    o_ref[...] = jnp.zeros_like(o_ref)

    def patch(buf, row, b, p0):
        lp = lens[b] - 1 - base

        @pl.when((lp >= p0) & (lp < p0 + CH))
        def _():
            buf[b, lp] = tr[:, row + b, :].astype(BF16)

    row = lax.broadcasted_iota(jnp.int32, (nh, CH * nh), 0)
    col = lax.broadcasted_iota(jnp.int32, (nh, CH * nh), 1)
    same = lax.rem(col, nh) == row

    def kstep(i, _):
        b = i // per
        p0 = pl.multiple_of(lax.rem(i, per) * CH, CH)
        rd(kc, kb, ki, i).wait()
        patch(kb, 2, b, p0)
        q = tr[:, b, :].astype(BF16)
        kk = kb[b, pl.ds(p0, CH)].reshape(CH * nh, dh)
        s = lax.dot_general(q, kk, (((1,), (1,)), ((), ())), preferred_element_type=F32) * dh ** -0.5
        lim = (lens[b] - base - p0) * nh
        s = jnp.where(same & (col < lim), s, -jnp.inf)
        s_ref[i] = s
        m_ref[b] = jnp.maximum(m_ref[b], jnp.max(s, axis=1, keepdims=True))
        wr(ko, kb, kos, i).start()
        return 0

    def vstep(i, _):
        b = i // per
        p0 = pl.multiple_of(lax.rem(i, per) * CH, CH)
        rd(vc, vb, vi, i).wait()
        patch(vb, 4, b, p0)
        m = m_ref[b][:, 0:1]
        m = jnp.where(m == -jnp.inf, 0.0, m)
        p = jnp.exp(s_ref[i] - m)
        l_ref[b] += jnp.sum(p, axis=1, keepdims=True)
        vv = vb[b, pl.ds(p0, CH)].reshape(CH * nh, dh)
        o_ref[b] += _dot(p.astype(BF16), vv)
        wr(vo, vb, vos, i).start()
        return 0

    lax.fori_loop(0, n, kstep, 0)
    lax.fori_loop(0, n, vstep, 0)
    lane = lax.broadcasted_iota(jnp.int32, (nh, dh), 1)
    for b in range(nb):
        ov = o_ref[b]
        ml = jnp.where(lane < 64, m_ref[b], l_ref[b])
        for r in range(8):
            op_ref[r, 0, b * 4:b * 4 + 4, :] = ov[4 * r:4 * r + 4]
            op_ref[r, 1, b * 4:b * 4 + 4, :] = ml[4 * r:4 * r + 4]
    for i in range(n):
        wr(ko, kb, kos, i).wait()
    for i in range(n):
        wr(vo, vb, vos, i).wait()


def solution(mesh):
    kspec = P(None, 'dp', 'sp', None, None)
    DMA = pltpu.SemaphoreType.DMA

    def local(x, lens, wq, wk, wv, wo, w1, w2, g1, g2, kc, vc):
        nl, nb, npos, nh, dh = kc.shape
        d = x.shape[1]
        h_sh = jax.ShapeDtypeStruct((8, d), F32)
        qkv_sh = jax.ShapeDtypeStruct((8, 8, NB), BF16)
        qkv_sc = [pltpu.VMEM((2, 8, NB), BF16), pltpu.VMEM((8, 8, NB), BF16)]
        cparams = lambda i, mib: pltpu.CompilerParams(
            collective_id=i, has_side_effects=True, vmem_limit_bytes=mib * 2 ** 20)

        h, qkv = pl.pallas_call(
            _first, out_shape=(h_sh, qkv_sh),
            in_specs=[VM, ANY, ANY, ANY, VM], out_specs=(VM, VM),
            scratch_shapes=[pltpu.VMEM((6, 2048, NB), BF16), pltpu.VMEM((2, d), BF16), *qkv_sc,
                            DMA((6,)), DMA, DMA, DMA((8,)), DMA((8,))],
            compiler_params=cparams(0, 40), name='first')(x, wq, wk, wv, g1)

        def attn(l, qkv, ko, vo):
            n = nb * npos // CH
            c_sh = jax.ShapeDtypeStruct(kc.shape, kc.dtype)
            args = [lens, qkv, kc, vc] + ([] if l == 0 else [ko, vo])
            return pl.pallas_call(
                functools.partial(_attn, l),
                out_shape=(c_sh, c_sh, jax.ShapeDtypeStruct((8, 2, 8, dh), F32)),
                in_specs=[SM, VM, ANY, ANY] + ([] if l == 0 else [ANY, ANY]),
                out_specs=(ANY, ANY, VM),
                scratch_shapes=[pltpu.VMEM((nb, npos, nh, dh), BF16), pltpu.VMEM((nb, npos, nh, dh), BF16),
                                pltpu.VMEM((nh, 8, dh), F32), pltpu.VMEM((n, nh, CH * nh), F32),
                                pltpu.VMEM((nb, nh, dh), F32), pltpu.VMEM((nb, nh, dh), F32),
                                pltpu.VMEM((nb, nh, dh), F32), DMA((n,)), DMA((n,)), DMA((n,)), DMA((n,))],
                input_output_aliases={} if l == 0 else {4: 0, 5: 1},
                compiler_params=pltpu.CompilerParams(vmem_limit_bytes=48 * 2 ** 20), name='attn')(*args)

        def layer(l, op, h, last):
            nw = 18 if last else 24
            sc = [pltpu.VMEM((nw, 2048, NB), BF16), pltpu.VMEM((8, 2, 8, dh), F32),
                  pltpu.VMEM((8, 512), F32), pltpu.VMEM((8, 2048), BF16),
                  pltpu.VMEM((2, 8, 1024), F32), pltpu.VMEM((2, 8, 1024), F32), pltpu.VMEM((2, 8, 1024), F32),
                  pltpu.VMEM((2, 4, 8, 1024), F32), pltpu.VMEM((2, 2, 8, 1024), F32),
                  DMA((30,)), DMA((8,)), DMA((8,)),
                  DMA((2,)), DMA((2,)), DMA((2, 4)), DMA((2, 4)), DMA((2,)), DMA((2,))]
            args = [op, h, wo, w1, w2, g2]
            specs = [VM, VM, ANY, ANY, ANY, VM]
            if last:
                sc = [pltpu.VMEM((8, d), F32)] + sc
                outs, out_specs = jax.ShapeDtypeStruct((nb, d), BF16), VM
            else:
                args += [wq, wk, wv, g1]
                specs += [ANY, ANY, ANY, VM]
                sc += qkv_sc + [DMA((8,)), DMA((8,))]
                outs, out_specs = (h_sh, qkv_sh), (VM, VM)
            return pl.pallas_call(
                functools.partial(_layer, l, last), out_shape=outs, in_specs=specs, out_specs=out_specs,
                scratch_shapes=sc, compiler_params=cparams(1 + l, 60), name='layer')(*args)

        ko = vo = None
        for l in range(nl):
            ko, vo, op = attn(l, qkv, ko, vo)
            if l < nl - 1:
                h, qkv = layer(l, op, h, False)
            else:
                y = layer(l, op, h, True)
        return y, ko, vo

    return jax.shard_map(
        local, mesh=mesh,
        in_specs=(P('dp', None), P('dp'), P(), P(), P(), P(None, 'sp', None), P(None, None, 'sp'),
                  P(None, 'sp', None), P(), P(), kspec, kspec),
        out_specs=(P('dp', None), kspec, kspec), check_vma=False)
```

time: 323 us -> 100 us (0.31); the launches traced: 317 us -> 100 us
  matrix products: 174 us -> 0 us
  Pallas kernels: 0 us -> 93.8 us
  blocking collectives: 78.9 us -> 0 us
  other arithmetic: 62.3 us -> 0 us
  local copies, waits for them, and re-layouts: 0.23 us -> 5.51 us
    dot_general x14 -> x0, matrix products: 174 us -> none  [the longest x10 134 us: _mm(): return jnp.dot(a, w, preferred_element_type=jnp.float32)]
    pallas_call x0 -> x5, Pallas kernels: none -> 93.8 us  [the longest x2 55.5 us: layer(): pl.pallas_call(functools.partial(_layer, l, last), out_shape=outs, in_spe...]
    psum x6 -> x0, blocking collectives: 63.4 us -> none  [the longest x2 21.5 us: local(): o, den = lax.psum((o * c[..., None], den * c), 'sp')]
    select_n x5 -> x0, other arithmetic: 36.7 us -> none  [the longest x3 36.7 us: local(): vl = jnp.where(write, v, vc[l])]
    another operation x2 -> x0, other arithmetic: 20.5 us -> none  [local(): return (h.astype(jnp.bfloat16), jnp.stack(ks), jnp.stack(vs))]
    pmax x2 -> x0, blocking collectives: 15.5 us -> none  [local(): c = jnp.exp(m - lax.pmax(m, 'sp'))]
    unnamed x6 -> x15, local copies, waits for them, and re-layouts: 0.02 us -> 5.51 us
where the time goes in v1:
time: 100 us
  Pallas kernels  93.8 us (94%)
  local copies, waits for them, and re-layouts  5.51 us (6%)
    pallas_call x2, Pallas kernels, layer(): pl.pallas_call(functools.partial(_layer, l, last), out_shape=outs, in_spe...  55.5 us
    pallas_call x2, Pallas kernels, attn(): pl.pallas_call(functools.partial(_attn, l), out_shape=(c_sh, c_sh, jax.Sh...  25.7 us
    pallas_call x1, Pallas kernels, local(): pl.pallas_call(_first, out_shape=(h_sh, qkv_sh), in_specs=[VM, ANY, ANY,...  12.6 us
    unnamed x15, local copies, waits for them, and re-layouts  5.51 us

profile of v1, /device:TPU:0, one launch (start us, length us, event | category | flops | bytes accessed | tf_op | source)
XLA Modules:
  0.0 100.0 jit_solution(3619371111281715166)
XLA Ops:
  0.6 0.0 copy-start.4
  0.6 0.7 copy-done.4
  1.4 0.0 copy-start.5
  1.4 0.7 copy-done.5
  2.1 0.0 copy-start.6
  2.1 12.6 %first.1 = (f32[8,4096]{1,0:T(8,128)S(1)}, bf16[8,8,512]{2,1,0:T(8,128)(2,1)S(1)}) custom-call(bf16[2,4096]{1,0:T(2,128)(2,1)S(1)} %copy-done.5, bf16[2,4096,4096]{2,1,0:T(8,128)(2,1)} %refs_6_.1, bf16[2,4096,4096]{2,1,0:T(8,128)(2,1)} %refs_7_.1, bf16[2,4096,4096]{2,1,0:T(8,128)(2,1)} %refs_8_.1, bf16[2,4096]{1,0:T(2,128)(2,1)S(1)} %copy-done.4), custom_call_target="tpu_custom_call" | custom-call | tf_op jit(solution)/shard_map/first/pallas_call | solution.py:338
  14.7 0.0 copy-start
  14.7 0.7 copy-done
  15.3 0.0 copy-done.6
  15.4 12.9 %attn.2 = (bf16[2,2,512,32,128]{4,3,2,1,0:T(8,128)(2,1)}, bf16[2,2,512,32,128]{4,3,2,1,0:T(8,128)(2,1)}, f32[8,2,8,128]{3,2,1,0:T(8,128)S(1)}) custom-call(s32[2]{0:T(128)S(1)} %copy-done.6, bf16[8,8,512]{2,1,0:T(8,128)(2,1)S(1)} %get-tuple-element.13.refs_1_, bf16[2,2,512,32,128]{4,3,2,1,0:T(8,128)(2,1)} %refs_2_.6, bf16[2,2,512,32,128]{4,3,2,1,0:T(8,128)(2,1)} %refs_3_.6), custom_call_target="tpu_custom_call" | custom-call | tf_op jit(solution)/shard_map/attn/pallas_call | solution.py:349
  28.2 0.0 copy-start.1
  28.2 0.6 copy-done.1
  28.9 30.9 %layer.2 = (f32[8,4096]{1,0:T(8,128)}, bf16[8,8,512]{2,1,0:T(8,128)(2,1)}) custom-call(f32[8,2,8,128]{3,2,1,0:T(8,128)} %copy-done.1, f32[8,4096]{1,0:T(8,128)} %copy-done, bf16[2,1024,4096]{2,1,0:T(8,128)(2,1)} %refs_2_.7, bf16[2,4096,4096]{2,1,0:T(8,128)(2,1)} %refs_3_.7, bf16[2,4096,4096]{2,1,0:T(8,128)(2,1)} %refs_4_.3, bf16[2,4096]{1,0:T(2,128)(2,1)} %refs_5_.3, ...), custom_call_target="tpu_custom_call" | custom-call | tf_op jit(solution)/shard_map/layer/pallas_call | solution.py:379
  59.7 0.0 copy-start.3
  59.7 0.8 copy-done.3
  60.6 12.9 %attn.3 = (bf16[2,2,512,32,128]{4,3,2,1,0:T(8,128)(2,1)}, bf16[2,2,512,32,128]{4,3,2,1,0:T(8,128)(2,1)}, f32[8,2,8,128]{3,2,1,0:T(8,128)S(1)}) custom-call(s32[2]{0:T(128)S(1)} %copy-done.6, bf16[8,8,512]{2,1,0:T(8,128)(2,1)S(1)} %copy-done.3, bf16[2,2,512,32,128]{4,3,2,1,0:T(8,128)(2,1)} %refs_2_.6, ...), custom_call_target="tpu_custom_call", output_to_operand_aliasing={{0}: (4, {}), {1}: (5, {})} | custom-call | tf_op jit(solution)/shard_map/attn/pallas_call | solution.py:349
  73.5 0.0 copy-start.2
  73.5 0.6 copy-done.2
  74.1 24.6 %layer.3 = bf16[2,4096]{1,0:T(2,128)(2,1)} custom-call(f32[8,2,8,128]{3,2,1,0:T(8,128)} %copy-done.2, f32[8,4096]{1,0:T(8,128)} %get-tuple-element.20.refs_1_, bf16[2,1024,4096]{2,1,0:T(8,128)(2,1)} %refs_2_.7, bf16[2,4096,4096]{2,1,0:T(8,128)(2,1)} %refs_3_.7, bf16[2,4096,4096]{2,1,0:T(8,128)(2,1)} %refs_4_.3, bf16[2,4096]{1,0:T(2,128)(2,1)} %refs_5_.3), custom_call_target="tpu_custom_call" | custom-call | tf_op jit(solution)/shard_map/layer/pallas_call | solution.py:379
  98.7 1.3 %copy.20 = bf16[2,4096]{1,0:T(2,128)(2,1)} copy(bf16[2,4096]{1,0:T(2,128)(2,1)} %layer.3) | data formatting | bytes 32768
Async XLA Ops:
  0.6 0.7 copy-start.4
  1.4 0.7 copy-start.5
  2.1 13.3 %copy-start.6 = (s32[2]{0:T(128)S(1)}, s32[2]{0:T(128)}, u32[]{:S(2)}) copy-start(s32[2]{0:T(128)} %refs_0_.3) | copy-start | bytes 28
  14.7 0.7 copy-start
  28.2 0.6 copy-start.1
  59.7 0.8 copy-start.3
  73.5 0.6 copy-start.2

commit v2 on v1

--- a/solution.py
+++ b/solution.py
@@ -10,11 +10,12 @@
 EPS = 1e-6
 MESH = pl.DeviceIdType.MESH
 VM = pl.BlockSpec(memory_space=pltpu.VMEM)
-ANY = pl.BlockSpec(memory_space=pl.ANY)
+ANY = pl.BlockSpec(memory_space=pltpu.HBM)
 SM = pl.BlockSpec(memory_space=pltpu.SMEM)
 F32, BF16 = jnp.float32, jnp.bfloat16
 CH = 128
 NB = 512
+LM = 39
 
 
 def _rms(h, g):
@@ -147,44 +148,59 @@
     qkv_ref[...] = recvA[...]
 
 
-def _first(x_ref, wq, wk, wv, g1, h_ref, qkv_ref, wbuf, xo, sendA, recvA, wsem, xs, xr, sa, ra):
+def _cache_copies(l, kc, vc, kb, vb, sem):
+    return [pltpu.make_async_copy(src.at[l, b], dst.at[b], sem.at[i, b])
+            for i, (src, dst) in enumerate(((kc, kb), (vc, vb))) for b in range(kb.shape[0])]
+
+
+def _first(x, wq, wk, wv, g1h, kc, vc, h_ref, qkv_ref, kb, vb,
+           wbuf, xm, xo, g1, sendA, recvA, wsem, xs, xr, sa, ra, gs, ks):
     dp, sp, c, me = _ids()
+    cs = [pltpu.make_async_copy(x, xm, gs.at[0]), pltpu.make_async_copy(g1h, g1, gs.at[1])]
     cq = _qkv_copies(0, me, (wq, wk, wv), wbuf, wsem, 0, 0)
-    for cp in cq:
+    ck = _cache_copies(0, kc, vc, kb, vb, ks)
+    for cp in cs + cq + ck:
         cp.start()
     _barrier(me)
-    ex = pltpu.make_async_remote_copy(x_ref, xo, xs, xr, device_id=(1 - dp, sp), device_id_type=MESH)
+    cs[0].wait()
+    ex = pltpu.make_async_remote_copy(xm, xo, xs, xr, device_id=(1 - dp, sp), device_id_type=MESH)
     ex.start()
+    cs[1].wait()
     ex.wait()
-    mine, other = x_ref[...].astype(F32), xo[...].astype(F32)
+    mine, other = xm[...].astype(F32), xo[...].astype(F32)
     h_ref[0:2, :] = jnp.where(dp == 0, mine, other)
     h_ref[2:4, :] = jnp.where(dp == 0, other, mine)
     h_ref[4:8, :] = jnp.zeros((4, h_ref.shape[1]), F32)
     xn = _rms(h_ref[...], g1[0:1, :])
     _qkv_stage(me, xn, wbuf, cq, 0, sendA, recvA, sa, ra, qkv_ref)
+    for cp in ck:
+        cp.wait()
 
 
 def _layer(l, last, *refs):
     if last:
-        (op_ref, hin, wo, w1, w2, g2, y_ref, h_ref, *sc) = refs
+        (op_ref, hin, wo, w1, w2, g2h, y_ref, h_ref, *sc) = refs
     else:
-        (op_ref, hin, wo, w1, w2, g2, wq, wk, wv, g1, h_ref, qkv_ref, *sc) = refs
-    wbuf, recvB, att, u, psend, pown, precv, chips, tot = sc[:9]
-    wsem, sb, rb, s1, r1, s2, r2, s3, r3 = sc[9:18]
+        (op_ref, hin, wo, w1, w2, g2h, wq, wk, wv, g1h, kc, vc, h_ref, qkv_ref, kb, vb, *sc) = refs
+    g2, gs, wbuf, recvB, att, u, psend, pown, precv, chips, tot = sc[:11]
+    wsem, sb, rb, s1, r1, s2, r2, s3, r3 = sc[11:20]
     dp, sp, c, me = _ids()
     cm = _mlp_copies(l, dp, c, wo, w1, w2, wbuf, wsem)
-    cq = []
+    cg = [pltpu.make_async_copy(g2h, g2, gs.at[0])]
+    ck = []
     if not last:
-        sendA, recvA, sa, ra = sc[18:]
-        cq = _qkv_copies(l + 1, me, (wq, wk, wv), wbuf, wsem, 18, 24)
-    for cp in cm + cq:
+        g1, sendA, recvA, sa, ra, ks = sc[20:]
+        cg.append(pltpu.make_async_copy(g1h, g1, gs.at[1]))
+        cq = _qkv_copies(l + 1, me, (wq, wk, wv), wbuf, wsem, 2, 24)
+        ck = _cache_copies(l + 1, kc, vc, kb, vb, ks)
+    for cp in cg + cm + ck:
         cp.start()
     _barrier(me)
     cps = _exchange(me, lambda d: op_ref.at[2 * lax.rem(d, 4) + d // 4], recvB.at[me], sb, rb)
     recvB[me] = op_ref[2 * sp + dp]
     h_ref[...] = hin[...]
     att[...] = jnp.zeros_like(att)
-    for cp in cps:
+    for cp in cg + cps:
         cp.wait()
     for g in range(2):
         ms = [recvB[4 * g + i, 1][:, 0:1] for i in range(4)]
@@ -221,6 +237,9 @@
         z = z + _dot(xn[:, 2048:], wbuf[3 + 2 * j])
         u[:, j * NB:(j + 1) * NB] = _gelu(z).astype(BF16)
     uv = u[...]
+    if not last:
+        for cp in cq:
+            cp.start()
 
     def w2_block(t, q):
         n = 2 * t + q
@@ -233,32 +252,28 @@
         y_ref[...] = jnp.where(dp == 0, hv[0:2], hv[2:4]).astype(BF16)
     else:
         xn = _rms(h_ref[...], g1[l + 1:l + 2, :])
-        _qkv_stage(me, xn, wbuf, cq, 18, sendA, recvA, sa, ra, qkv_ref)
+        _qkv_stage(me, xn, wbuf, cq, 2, sendA, recvA, sa, ra, qkv_ref)
+        for cp in ck:
+            cp.wait()
 
 
 def _attn(l, *refs):
     if l == 0:
-        lens, qkv, kc, vc, ko, vo, op_ref, *sc = refs
+        lensh, qkv, kin, vin, ko, vo, op_ref, kb, vb, *sc = refs
     else:
-        lens, qkv, kc, vc, _, _, ko, vo, op_ref, *sc = refs
-    kb, vb, tr, s_ref, m_ref, l_ref, o_ref, ki, vi, kos, vos = sc
+        lensh, qkv, kin, vin, _, _, ko, vo, op_ref, kb, vb, *sc = refs
+    lens, tr, s_ref, m_ref, l_ref, o_ref, ls, kos, vos = sc
     nb, npos, nh, dh = kb.shape
     per = npos // CH
     n = nb * per
     base = lax.axis_index('sp') * npos
-
-    def rd(src, buf, sem, i):
-        b, p = i // per, pl.multiple_of(lax.rem(i, per) * CH, CH)
-        return pltpu.make_async_copy(src.at[l, b, pl.ds(p, CH)], buf.at[b, pl.ds(p, CH)], sem.at[i])
+    cl = pltpu.make_async_copy(lensh, lens, ls)
+    cl.start()
 
     def wr(dst, buf, sem, i):
         b, p = i // per, pl.multiple_of(lax.rem(i, per) * CH, CH)
         return pltpu.make_async_copy(buf.at[b, pl.ds(p, CH)], dst.at[l, b, pl.ds(p, CH)], sem.at[i])
 
-    for i in range(n):
-        rd(kc, kb, ki, i).start()
-    for i in range(n):
-        rd(vc, vb, vi, i).start()
     for src in range(8):
         v = qkv[src].astype(F32)
         for j in range(4):
@@ -266,13 +281,14 @@
     m_ref[...] = jnp.full(m_ref.shape, -jnp.inf, F32)
     l_ref[...] = jnp.zeros_like(l_ref)
     o_ref[...] = jnp.zeros_like(o_ref)
-
-    def patch(buf, row, b, p0):
+    cl.wait()
+    for b in range(nb):
         lp = lens[b] - 1 - base
 
-        @pl.when((lp >= p0) & (lp < p0 + CH))
+        @pl.when((lp >= 0) & (lp < npos))
         def _():
-            buf[b, lp] = tr[:, row + b, :].astype(BF16)
+            kb[b, lp] = tr[:, 2 + b, :].astype(BF16)
+            vb[b, lp] = tr[:, 4 + b, :].astype(BF16)
 
     row = lax.broadcasted_iota(jnp.int32, (nh, CH * nh), 0)
     col = lax.broadcasted_iota(jnp.int32, (nh, CH * nh), 1)
@@ -281,8 +297,6 @@
     def kstep(i, _):
         b = i // per
         p0 = pl.multiple_of(lax.rem(i, per) * CH, CH)
-        rd(kc, kb, ki, i).wait()
-        patch(kb, 2, b, p0)
         q = tr[:, b, :].astype(BF16)
         kk = kb[b, pl.ds(p0, CH)].reshape(CH * nh, dh)
         s = lax.dot_general(q, kk, (((1,), (1,)), ((), ())), preferred_element_type=F32) * dh ** -0.5
@@ -291,20 +305,18 @@
         s_ref[i] = s
         m_ref[b] = jnp.maximum(m_ref[b], jnp.max(s, axis=1, keepdims=True))
         wr(ko, kb, kos, i).start()
+        wr(vo, vb, vos, i).start()
         return 0
 
     def vstep(i, _):
         b = i // per
         p0 = pl.multiple_of(lax.rem(i, per) * CH, CH)
-        rd(vc, vb, vi, i).wait()
-        patch(vb, 4, b, p0)
         m = m_ref[b][:, 0:1]
         m = jnp.where(m == -jnp.inf, 0.0, m)
         p = jnp.exp(s_ref[i] - m)
         l_ref[b] += jnp.sum(p, axis=1, keepdims=True)
         vv = vb[b, pl.ds(p0, CH)].reshape(CH * nh, dh)
         o_ref[b] += _dot(p.astype(BF16), vv)
-        wr(vo, vb, vos, i).start()
         return 0
 
     lax.fori_loop(0, n, kstep, 0)
@@ -318,7 +330,6 @@
             op_ref[r, 1, b * 4:b * 4 + 4, :] = ml[4 * r:4 * r + 4]
     for i in range(n):
         wr(ko, kb, kos, i).wait()
-    for i in range(n):
         wr(vo, vb, vos, i).wait()
 
 
@@ -329,62 +340,66 @@
     def local(x, lens, wq, wk, wv, wo, w1, w2, g1, g2, kc, vc):
         nl, nb, npos, nh, dh = kc.shape
         d = x.shape[1]
-        h_sh = jax.ShapeDtypeStruct((8, d), F32)
-        qkv_sh = jax.ShapeDtypeStruct((8, 8, NB), BF16)
-        qkv_sc = [pltpu.VMEM((2, 8, NB), BF16), pltpu.VMEM((8, 8, NB), BF16)]
+        V = lambda *sh_dt: pltpu.VMEM(*sh_dt)
+        hbm = lambda *xs: [pltpu.with_memory_space_constraint(a, pltpu.HBM) for a in xs]
+        vm = lambda *xs: [pltpu.with_memory_space_constraint(a, pltpu.VMEM) for a in xs]
+        h_sh, qkv_sh = V((8, d), F32), V((8, 8, NB), BF16)
+        c_vm = V((nb, npos, nh, dh), BF16)
+        qkv_sc = [V((2, 8, NB), BF16), V((8, 8, NB), BF16)]
         cparams = lambda i, mib: pltpu.CompilerParams(
             collective_id=i, has_side_effects=True, vmem_limit_bytes=mib * 2 ** 20)
 
-        h, qkv = pl.pallas_call(
-            _first, out_shape=(h_sh, qkv_sh),
-            in_specs=[VM, ANY, ANY, ANY, VM], out_specs=(VM, VM),
-            scratch_shapes=[pltpu.VMEM((6, 2048, NB), BF16), pltpu.VMEM((2, d), BF16), *qkv_sc,
-                            DMA((6,)), DMA, DMA, DMA((8,)), DMA((8,))],
-            compiler_params=cparams(0, 40), name='first')(x, wq, wk, wv, g1)
-
-        def attn(l, qkv, ko, vo):
+        h, qkv, kb, vb = pl.pallas_call(
+            _first, out_shape=(h_sh, qkv_sh, c_vm, c_vm),
+            in_specs=[ANY] * 7, out_specs=(VM,) * 4,
+            scratch_shapes=[V((6, 2048, NB), BF16), V((2, d), BF16), V((2, d), BF16), V((nl, d), BF16), *qkv_sc,
+                            DMA((6,)), DMA, DMA, DMA((8,)), DMA((8,)), DMA((2,)), DMA((2, nb))],
+            compiler_params=cparams(0, 16), name='first')(*hbm(x, wq, wk, wv, g1, kc, vc))
+
+        def attn(l, qkv, kb, vb, ko, vo):
             n = nb * npos // CH
             c_sh = jax.ShapeDtypeStruct(kc.shape, kc.dtype)
-            args = [lens, qkv, kc, vc] + ([] if l == 0 else [ko, vo])
+            args = hbm(lens) + vm(qkv, kb, vb) + ([] if l == 0 else hbm(ko, vo))
+            al = {2: 3, 3: 4}
+            if l > 0:
+                al.update({4: 0, 5: 1})
             return pl.pallas_call(
                 functools.partial(_attn, l),
-                out_shape=(c_sh, c_sh, jax.ShapeDtypeStruct((8, 2, 8, dh), F32)),
-                in_specs=[SM, VM, ANY, ANY] + ([] if l == 0 else [ANY, ANY]),
-                out_specs=(ANY, ANY, VM),
-                scratch_shapes=[pltpu.VMEM((nb, npos, nh, dh), BF16), pltpu.VMEM((nb, npos, nh, dh), BF16),
-                                pltpu.VMEM((nh, 8, dh), F32), pltpu.VMEM((n, nh, CH * nh), F32),
-                                pltpu.VMEM((nb, nh, dh), F32), pltpu.VMEM((nb, nh, dh), F32),
-                                pltpu.VMEM((nb, nh, dh), F32), DMA((n,)), DMA((n,)), DMA((n,)), DMA((n,))],
-                input_output_aliases={} if l == 0 else {4: 0, 5: 1},
-                compiler_params=pltpu.CompilerParams(vmem_limit_bytes=48 * 2 ** 20), name='attn')(*args)
+                out_shape=(c_sh, c_sh, V((8, 2, 8, dh), F32), c_vm, c_vm),
+                in_specs=[ANY, VM, VM, VM] + ([] if l == 0 else [ANY, ANY]),
+                out_specs=(ANY, ANY, VM, VM, VM),
+                scratch_shapes=[pltpu.SMEM((nb,), jnp.int32), V((nh, 8, dh), F32), V((n, nh, CH * nh), F32),
+                                V((nb, nh, dh), F32), V((nb, nh, dh), F32), V((nb, nh, dh), F32),
+                                DMA, DMA((n,)), DMA((n,))],
+                input_output_aliases=al,
+                compiler_params=pltpu.CompilerParams(vmem_limit_bytes=14 * 2 ** 20), name='attn')(*args)[:3]
 
         def layer(l, op, h, last):
-            nw = 18 if last else 24
-            sc = [pltpu.VMEM((nw, 2048, NB), BF16), pltpu.VMEM((8, 2, 8, dh), F32),
-                  pltpu.VMEM((8, 512), F32), pltpu.VMEM((8, 2048), BF16),
-                  pltpu.VMEM((2, 8, 1024), F32), pltpu.VMEM((2, 8, 1024), F32), pltpu.VMEM((2, 8, 1024), F32),
-                  pltpu.VMEM((2, 4, 8, 1024), F32), pltpu.VMEM((2, 2, 8, 1024), F32),
+            sc = [V((nl, d), BF16), DMA((2,)), V((18, 2048, NB), BF16), V((8, 2, 8, dh), F32),
+                  V((8, 512), F32), V((8, 2048), BF16),
+                  V((2, 8, 1024), F32), V((2, 8, 1024), F32), V((2, 8, 1024), F32),
+                  V((2, 4, 8, 1024), F32), V((2, 2, 8, 1024), F32),
                   DMA((30,)), DMA((8,)), DMA((8,)),
                   DMA((2,)), DMA((2,)), DMA((2, 4)), DMA((2, 4)), DMA((2,)), DMA((2,))]
-            args = [op, h, wo, w1, w2, g2]
-            specs = [VM, VM, ANY, ANY, ANY, VM]
+            args = vm(op, h) + hbm(wo, w1, w2, g2)
+            specs = [VM, VM, ANY, ANY, ANY, ANY]
             if last:
-                sc = [pltpu.VMEM((8, d), F32)] + sc
-                outs, out_specs = jax.ShapeDtypeStruct((nb, d), BF16), VM
+                sc = [V((8, d), F32)] + sc
+                outs, out_specs, mib = jax.ShapeDtypeStruct((nb, d), BF16), VM, 39
             else:
-                args += [wq, wk, wv, g1]
-                specs += [ANY, ANY, ANY, VM]
-                sc += qkv_sc + [DMA((8,)), DMA((8,))]
-                outs, out_specs = (h_sh, qkv_sh), (VM, VM)
+                args += hbm(wq, wk, wv, g1, kc, vc)
+                specs += [ANY] * 6
+                sc += [V((nl, d), BF16), *qkv_sc, DMA((8,)), DMA((8,)), DMA((2, nb))]
+                outs, out_specs, mib = (h_sh, qkv_sh, c_vm, c_vm), (VM,) * 4, LM
             return pl.pallas_call(
                 functools.partial(_layer, l, last), out_shape=outs, in_specs=specs, out_specs=out_specs,
-                scratch_shapes=sc, compiler_params=cparams(1 + l, 60), name='layer')(*args)
+                scratch_shapes=sc, compiler_params=cparams(1 + l, mib), name='layer')(*args)
 
         ko = vo = None
         for l in range(nl):
-            ko, vo, op = attn(l, qkv, ko, vo)
+            ko, vo, op = attn(l, qkv, kb, vb, ko, vo)
             if l < nl - 1:
-                h, qkv = layer(l, op, h, False)
+                h, qkv, kb, vb = layer(l, op, h, False)
             else:
                 y = layer(l, op, h, True)
         return y, ko, vo

time: 100 us -> 105 us (1.050)
  Pallas kernels: 93.8 us -> 103 us
  local copies, waits for them, and re-layouts: 5.51 us -> 0.61 us
    pallas_call x2, Pallas kernels: 55.5 us -> 69.5 us  [layer(): pl.pallas_call(functools.partial(_layer, l, last), out_shape=outs, in_spe...]
    unnamed x15 -> x1, local copies, waits for them, and re-layouts: 5.51 us -> 0.61 us
    pallas_call x3, Pallas kernels: 38.3 us -> 33.8 us  [the longest x2 17 us: attn(): pl.pallas_call(functools.partial(_attn, l), out_shape=(c_sh, c_sh, V((8,...]
where the time goes in v2:
time: 105 us
  Pallas kernels  103 us (98%)
    pallas_call x2, Pallas kernels, layer(): pl.pallas_call(functools.partial(_layer, l, last), out_shape=outs, in_spe...  69.5 us
    pallas_call x2, Pallas kernels, attn(): pl.pallas_call(functools.partial(_attn, l), out_shape=(c_sh, c_sh, V((8,...  17 us
    pallas_call x1, Pallas kernels, local(): pl.pallas_call(_first, out_shape=(h_sh, qkv_sh, c_vm, c_vm), in_specs=[AN...  16.8 us

profile of v2, /device:TPU:0, one launch (start us, length us, event | category | flops | bytes accessed | tf_op | source)
XLA Modules:
  0.0 104.6 jit_solution(9790112223897961821)
XLA Ops:
  0.6 16.8 %first.1 = (f32[8,4096]{1,0:T(8,128)S(1)}, bf16[8,8,512]{2,1,0:T(8,128)(2,1)S(1)}, bf16[2,512,32,128]{3,2,1,0:T(8,128)(2,1)S(1)}, bf16[2,512,32,128]{3,2,1,0:T(8,128)(2,1)S(1)}) custom-call(bf16[2,4096]{1,0:T(2,128)(2,1)} %x.1, bf16[2,4096,4096]{2,1,0:T(8,128)(2,1)} %refs_6_.1, bf16[2,4096,4096]{2,1,0:T(8,128)(2,1)} %refs_7_.1, ...), custom_call_target="tpu_custom_call" | custom-call | tf_op jit(solution)/shard_map/first/pallas_call | solution.py:352
  17.5 8.4 %attn.2 = (bf16[2,2,512,32,128]{4,3,2,1,0:T(8,128)(2,1)}, bf16[2,2,512,32,128]{4,3,2,1,0:T(8,128)(2,1)}, f32[8,2,8,128]{3,2,1,0:T(8,128)S(1)}, bf16[2,512,32,128...) custom-call(s32[2]{0:T(128)} %refs_0_.3, ...), custom_call_target="tpu_custom_call", output_to_operand_aliasing={{3}: (2, {}), {4}: (3, {})} | custom-call | tf_op jit(solution)/shard_map/attn/pallas_call | solution.py:366
  25.9 39.2 %layer.2 = (f32[8,4096]{1,0:T(8,128)S(1)}, bf16[8,8,512]{2,1,0:T(8,128)(2,1)S(1)}, bf16[2,512,32,128]{3,2,1,0:T(8,128)(2,1)S(1)}, bf16[2,512,32,128]{3,2,1,0:T(8,128)(2,1)S(1)}) custom-call(f32[8,2,8,128]{3,2,1,0:T(8,128)S(1)} %get-tuple-element.20.refs_0_, f32[8,4096]{1,0:T(8,128)S(1)} %get-tuple-element.21.refs_1_, bf16[2,1024,4096]{2,1,0:T(8,128)(2,1)} %refs_2_.3, ...), custom_call_target="tpu_custom_call" | custom-call | tf_op jit(solution)/shard_map/layer/pallas_call | solution.py:394
  65.1 8.6 %attn.3 = (bf16[2,2,512,32,128]{4,3,2,1,0:T(8,128)(2,1)}, bf16[2,2,512,32,128]{4,3,2,1,0:T(8,128)(2,1)}, f32[8,2,8,128]{3,2,1,0:T(8,128)S(1)}, bf16[2,512,32,128...) custom-call(s32[2]{0:T(128)} %refs_0_.3, ...), custom_call_target="tpu_custom_call", output_to_operand_aliasing={{3}: (2, {}), {4}: (3, {}), {0}: (4, {}), {1}: (5, {})} | custom-call | tf_op jit(solution)/shard_map/attn/pallas_call | solution.py:366
  73.7 30.3 %layer.3 = bf16[2,4096]{1,0:T(2,128)(2,1)S(1)} custom-call(f32[8,2,8,128]{3,2,1,0:T(8,128)S(1)} %get-tuple-element.27.refs_0_, f32[8,4096]{1,0:T(8,128)S(1)} %get-tuple-element.28.refs_1_, bf16[2,1024,4096]{2,1,0:T(8,128)(2,1)} %refs_2_.3, bf16[2,4096,4096]{2,1,0:T(8,128)(2,1)} %refs_3_.3, bf16[2,4096,4096]{2,1,0:T(8,128)(2,1)} %refs_4_.3, ...), custom_call_target="tpu_custom_call" | custom-call | tf_op jit(solution)/shard_map/layer/pallas_call | solution.py:394
  104.0 0.6 copy.28

commit v3 on v2

--- a/solution.py
+++ b/solution.py
@@ -153,25 +153,24 @@
             for i, (src, dst) in enumerate(((kc, kb), (vc, vb))) for b in range(kb.shape[0])]
 
 
-def _first(x, wq, wk, wv, g1h, kc, vc, h_ref, qkv_ref, kb, vb,
-           wbuf, xm, xo, g1, sendA, recvA, wsem, xs, xr, sa, ra, gs, ks):
+def _first(xm, wq, wk, wv, g1, kc, vc, h_ref, qkv_ref, kb, vb,
+           wbuf, xo, sendA, recvA, wsem, xs, xr, sa, ra, ks):
     dp, sp, c, me = _ids()
-    cs = [pltpu.make_async_copy(x, xm, gs.at[0]), pltpu.make_async_copy(g1h, g1, gs.at[1])]
     cq = _qkv_copies(0, me, (wq, wk, wv), wbuf, wsem, 0, 0)
     ck = _cache_copies(0, kc, vc, kb, vb, ks)
-    for cp in cs + cq + ck:
+    for cp in cq:
         cp.start()
     _barrier(me)
-    cs[0].wait()
     ex = pltpu.make_async_remote_copy(xm, xo, xs, xr, device_id=(1 - dp, sp), device_id_type=MESH)
     ex.start()
-    cs[1].wait()
     ex.wait()
     mine, other = xm[...].astype(F32), xo[...].astype(F32)
     h_ref[0:2, :] = jnp.where(dp == 0, mine, other)
     h_ref[2:4, :] = jnp.where(dp == 0, other, mine)
     h_ref[4:8, :] = jnp.zeros((4, h_ref.shape[1]), F32)
     xn = _rms(h_ref[...], g1[0:1, :])
+    for cp in ck:
+        cp.start()
     _qkv_stage(me, xn, wbuf, cq, 0, sendA, recvA, sa, ra, qkv_ref)
     for cp in ck:
         cp.wait()
@@ -179,28 +178,26 @@
 
 def _layer(l, last, *refs):
     if last:
-        (op_ref, hin, wo, w1, w2, g2h, y_ref, h_ref, *sc) = refs
+        (op_ref, hin, wo, w1, w2, g2, y_ref, h_ref, *sc) = refs
     else:
-        (op_ref, hin, wo, w1, w2, g2h, wq, wk, wv, g1h, kc, vc, h_ref, qkv_ref, kb, vb, *sc) = refs
-    g2, gs, wbuf, recvB, att, u, psend, pown, precv, chips, tot = sc[:11]
-    wsem, sb, rb, s1, r1, s2, r2, s3, r3 = sc[11:20]
+        (op_ref, hin, wo, w1, w2, g2, wq, wk, wv, g1, kc, vc, h_ref, qkv_ref, kb, vb, *sc) = refs
+    wbuf, recvB, att, u, psend, pown, precv, chips, tot = sc[:9]
+    wsem, sb, rb, s1, r1, s2, r2, s3, r3 = sc[9:18]
     dp, sp, c, me = _ids()
     cm = _mlp_copies(l, dp, c, wo, w1, w2, wbuf, wsem)
-    cg = [pltpu.make_async_copy(g2h, g2, gs.at[0])]
     ck = []
     if not last:
-        g1, sendA, recvA, sa, ra, ks = sc[20:]
-        cg.append(pltpu.make_async_copy(g1h, g1, gs.at[1]))
+        sendA, recvA, sa, ra, ks = sc[18:]
         cq = _qkv_copies(l + 1, me, (wq, wk, wv), wbuf, wsem, 2, 24)
         ck = _cache_copies(l + 1, kc, vc, kb, vb, ks)
-    for cp in cg + cm + ck:
+    for cp in cm + ck:
         cp.start()
     _barrier(me)
     cps = _exchange(me, lambda d: op_ref.at[2 * lax.rem(d, 4) + d // 4], recvB.at[me], sb, rb)
     recvB[me] = op_ref[2 * sp + dp]
     h_ref[...] = hin[...]
     att[...] = jnp.zeros_like(att)
-    for cp in cg + cps:
+    for cp in cps:
         cp.wait()
     for g in range(2):
         ms = [recvB[4 * g + i, 1][:, 0:1] for i in range(4)]
@@ -351,10 +348,10 @@
 
         h, qkv, kb, vb = pl.pallas_call(
             _first, out_shape=(h_sh, qkv_sh, c_vm, c_vm),
-            in_specs=[ANY] * 7, out_specs=(VM,) * 4,
-            scratch_shapes=[V((6, 2048, NB), BF16), V((2, d), BF16), V((2, d), BF16), V((nl, d), BF16), *qkv_sc,
-                            DMA((6,)), DMA, DMA, DMA((8,)), DMA((8,)), DMA((2,)), DMA((2, nb))],
-            compiler_params=cparams(0, 16), name='first')(*hbm(x, wq, wk, wv, g1, kc, vc))
+            in_specs=[VM, ANY, ANY, ANY, VM, ANY, ANY], out_specs=(VM,) * 4,
+            scratch_shapes=[V((6, 2048, NB), BF16), V((2, d), BF16), *qkv_sc,
+                            DMA((6,)), DMA, DMA, DMA((8,)), DMA((8,)), DMA((2, nb))],
+            compiler_params=cparams(0, 16), name='first')(*(vm(x) + hbm(wq, wk, wv) + vm(g1) + hbm(kc, vc)))
 
         def attn(l, qkv, kb, vb, ko, vo):
             n = nb * npos // CH
@@ -375,21 +372,21 @@
                 compiler_params=pltpu.CompilerParams(vmem_limit_bytes=14 * 2 ** 20), name='attn')(*args)[:3]
 
         def layer(l, op, h, last):
-            sc = [V((nl, d), BF16), DMA((2,)), V((18, 2048, NB), BF16), V((8, 2, 8, dh), F32),
+            sc = [V((18, 2048, NB), BF16), V((8, 2, 8, dh), F32),
                   V((8, 512), F32), V((8, 2048), BF16),
                   V((2, 8, 1024), F32), V((2, 8, 1024), F32), V((2, 8, 1024), F32),
                   V((2, 4, 8, 1024), F32), V((2, 2, 8, 1024), F32),
                   DMA((30,)), DMA((8,)), DMA((8,)),
                   DMA((2,)), DMA((2,)), DMA((2, 4)), DMA((2, 4)), DMA((2,)), DMA((2,))]
-            args = vm(op, h) + hbm(wo, w1, w2, g2)
-            specs = [VM, VM, ANY, ANY, ANY, ANY]
+            args = vm(op, h) + hbm(wo, w1, w2) + vm(g2)
+            specs = [VM, VM, ANY, ANY, ANY, VM]
             if last:
                 sc = [V((8, d), F32)] + sc
                 outs, out_specs, mib = jax.ShapeDtypeStruct((nb, d), BF16), VM, 39
             else:
-                args += hbm(wq, wk, wv, g1, kc, vc)
-                specs += [ANY] * 6
-                sc += [V((nl, d), BF16), *qkv_sc, DMA((8,)), DMA((8,)), DMA((2, nb))]
+                args += hbm(wq, wk, wv) + vm(g1) + hbm(kc, vc)
+                specs += [ANY, ANY, ANY, VM, ANY, ANY]
+                sc += [*qkv_sc, DMA((8,)), DMA((8,)), DMA((2, nb))]
                 outs, out_specs, mib = (h_sh, qkv_sh, c_vm, c_vm), (VM,) * 4, LM
             return pl.pallas_call(
                 functools.partial(_layer, l, last), out_shape=outs, in_specs=specs, out_specs=out_specs,

time: 105 us -> 85.3 us (0.81)
  Pallas kernels: 103 us -> 82.2 us
  local copies, waits for them, and re-layouts: 0.61 us -> 2.05 us
    pallas_call x2, Pallas kernels: 69.5 us -> 52.4 us  [layer(): pl.pallas_call(functools.partial(_layer, l, last), out_shape=outs, in_spe...]
    pallas_call x1, Pallas kernels: 16.8 us -> 12.7 us  [local(): pl.pallas_call(_first, out_shape=(h_sh, qkv_sh, c_vm, c_vm), in_specs=[VM...]
    unnamed x1 -> x9, local copies, waits for them, and re-layouts: 0.61 us -> 2.05 us
where the time goes in v3:
time: 85.3 us; the launch traced here: 85 us
  Pallas kernels  82.2 us (96%)
  local copies, waits for them, and re-layouts  2.05 us (2%)
    pallas_call x2, Pallas kernels, layer(): pl.pallas_call(functools.partial(_layer, l, last), out_shape=outs, in_spe...  52.4 us
    pallas_call x2, Pallas kernels, attn(): pl.pallas_call(functools.partial(_attn, l), out_shape=(c_sh, c_sh, V((8,...  17.1 us
    pallas_call x1, Pallas kernels, local(): pl.pallas_call(_first, out_shape=(h_sh, qkv_sh, c_vm, c_vm), in_specs=[VM...  12.7 us
    unnamed x9, local copies, waits for them, and re-layouts  2.05 us

profile of v3, /device:TPU:0, one launch (start us, length us, event | category | flops | bytes accessed | tf_op | source)
XLA Modules:
  0.0 85.0 jit_solution(13742770343863312599)
XLA Ops:
  0.6 0.0 copy-start
  0.6 0.7 copy-done
  1.4 0.0 copy-start.3
  1.4 0.7 copy-done.3
  2.1 12.7 %first.1 = (f32[8,4096]{1,0:T(8,128)S(1)}, bf16[8,8,512]{2,1,0:T(8,128)(2,1)S(1)}, bf16[2,512,32,128]{3,2,1,0:T(8,128)(2,1)S(1)}, bf16[2,512,32,128]{3,2,1,0:T(8,128)(2,1)S(1)}) custom-call(bf16[2,4096]{1,0:T(2,128)(2,1)S(1)} %copy-done.3, bf16[2,4096,4096]{2,1,0:T(8,128)(2,1)} %refs_6_.1, bf16[2,4096,4096]{2,1,0:T(8,128)(2,1)} %refs_7_.1, ...), custom_call_target="tpu_custom_call" | custom-call | tf_op jit(solution)/shard_map/first/pallas_call | solution.py:349
  14.8 0.0 copy-start.1
  14.8 0.0 copy-start.2
  14.8 8.5 %attn.2 = (bf16[2,2,512,32,128]{4,3,2,1,0:T(8,128)(2,1)}, bf16[2,2,512,32,128]{4,3,2,1,0:T(8,128)(2,1)}, f32[8,2,8,128]{3,2,1,0:T(8,128)S(1)}, bf16[2,512,32,128...) custom-call(s32[2]{0:T(128)} %refs_0_.3, ...), custom_call_target="tpu_custom_call", output_to_operand_aliasing={{3}: (2, {}), {4}: (3, {})} | custom-call | tf_op jit(solution)/shard_map/attn/pallas_call | solution.py:363
  23.3 0.0 copy-done.1
  23.3 0.0 copy-done.2
  23.4 29.3 %layer.2 = (f32[8,4096]{1,0:T(8,128)S(1)}, bf16[8,8,512]{2,1,0:T(8,128)(2,1)S(1)}, bf16[2,512,32,128]{3,2,1,0:T(8,128)(2,1)S(1)}, bf16[2,512,32,128]{3,2,1,0:T(8,128)(2,1)S(1)}) custom-call(f32[8,2,8,128]{3,2,1,0:T(8,128)S(1)} %get-tuple-element.20.refs_0_, f32[8,4096]{1,0:T(8,128)S(1)} %get-tuple-element.21.refs_1_, bf16[2,1024,4096]{2,1,0:T(8,128)(2,1)} %refs_2_.3, ...), custom_call_target="tpu_custom_call" | custom-call | tf_op jit(solution)/shard_map/layer/pallas_call | solution.py:391
  52.7 8.6 %attn.3 = (bf16[2,2,512,32,128]{4,3,2,1,0:T(8,128)(2,1)}, bf16[2,2,512,32,128]{4,3,2,1,0:T(8,128)(2,1)}, f32[8,2,8,128]{3,2,1,0:T(8,128)S(1)}, bf16[2,512,32,128...) custom-call(s32[2]{0:T(128)} %refs_0_.3, ...), custom_call_target="tpu_custom_call", output_to_operand_aliasing={{3}: (2, {}), {4}: (3, {}), {0}: (4, {}), {1}: (5, {})} | custom-call | tf_op jit(solution)/shard_map/attn/pallas_call | solution.py:363
  61.2 23.1 %layer.3 = bf16[2,4096]{1,0:T(2,128)(2,1)S(1)} custom-call(f32[8,2,8,128]{3,2,1,0:T(8,128)S(1)} %get-tuple-element.27.refs_0_, f32[8,4096]{1,0:T(8,128)S(1)} %get-tuple-element.28.refs_1_, bf16[2,1024,4096]{2,1,0:T(8,128)(2,1)} %refs_2_.3, bf16[2,4096,4096]{2,1,0:T(8,128)(2,1)} %refs_3_.3, bf16[2,4096,4096]{2,1,0:T(8,128)(2,1)} %refs_4_.3, ...), custom_call_target="tpu_custom_call" | custom-call | tf_op jit(solution)/shard_map/layer/pallas_call | solution.py:391
  84.4 0.6 copy.28
Async XLA Ops:
  0.6 0.7 copy-start
  1.4 0.7 copy-start.3
  14.8 8.6 %copy-start.1 = (bf16[2,4096]{1,0:T(2,128)(2,1)S(1)}, bf16[2,4096]{1,0:T(2,128)(2,1)}, u32[]{:S(2)}) copy-start(bf16[2,4096]{1,0:T(2,128)(2,1)} %refs_9_.1) | copy-start | bytes 49156
  14.8 8.6 %copy-start.2 = (bf16[2,4096]{1,0:T(2,128)(2,1)S(1)}, bf16[2,4096]{1,0:T(2,128)(2,1)}, u32[]{:S(2)}) copy-start(bf16[2,4096]{1,0:T(2,128)(2,1)} %refs_5_.3) | copy-start | bytes 49156

commit v4 on v3

--- a/solution.py
+++ b/solution.py
@@ -36,12 +36,15 @@
     return dp, sp, lax.rem(sp, 2), dp * 4 + sp
 
 
-def _barrier(me):
+def _hello(me):
     sem = pltpu.get_barrier_semaphore()
     for k in range(1, 8):
         d = lax.rem(me + k, 8)
         pl.semaphore_signal(sem, inc=1, device_id=(d // 4, lax.rem(d, 4)), device_id_type=MESH)
-    pl.semaphore_wait(sem, 7)
+
+
+def _barrier():
+    pl.semaphore_wait(pltpu.get_barrier_semaphore(), 7)
 
 
 def _exchange(me, src, dst, ssem, rsem):
@@ -130,12 +133,14 @@
             h_ref[0:4, lo:lo + 1024] += tot[half, q * 4:q * 4 + 4, :]
 
 
-def _qkv_stage(me, xn, wbuf, copies, slot, sendA, recvA, ssem, rsem, qkv_ref):
+def _qkv_stage(chase, me, xn, wbuf, copies, slot, sendA, recvA, ssem, rsem, qkv_ref):
     res = []
+    step = 2 if chase else 6
     for i in range(3):
-        copies[2 * i].wait()
+        if 2 * i % step == 0:
+            for cp in copies[2 * i:2 * i + step]:
+                cp.wait()
         z = _dot(xn[:, :2048], wbuf[slot + 2 * i])
-        copies[2 * i + 1].wait()
         z = z + _dot(xn[:, 2048:], wbuf[slot + 2 * i + 1])
         res.append(z)
     for g in range(2):
@@ -153,14 +158,20 @@
             for i, (src, dst) in enumerate(((kc, kb), (vc, vb))) for b in range(kb.shape[0])]
 
 
-def _first(xm, wq, wk, wv, g1, kc, vc, h_ref, qkv_ref, kb, vb,
-           wbuf, xo, sendA, recvA, wsem, xs, xr, sa, ra, ks):
+def _first(x, wq, wk, wv, g1h, kc, vc, h_ref, qkv_ref, kb, vb,
+           wbuf, xm, xo, g1, sendA, recvA, wsem, xs, xr, sa, ra, gs, ks):
     dp, sp, c, me = _ids()
     cq = _qkv_copies(0, me, (wq, wk, wv), wbuf, wsem, 0, 0)
     ck = _cache_copies(0, kc, vc, kb, vb, ks)
+    _hello(me)
+    cs = [pltpu.make_async_copy(x, xm, gs.at[0]), pltpu.make_async_copy(g1h, g1, gs.at[1])]
+    for cp in cs:
+        cp.start()
+    for cp in cs:
+        cp.wait()
     for cp in cq:
         cp.start()
-    _barrier(me)
+    _barrier()
     ex = pltpu.make_async_remote_copy(xm, xo, xs, xr, device_id=(1 - dp, sp), device_id_type=MESH)
     ex.start()
     ex.wait()
@@ -171,7 +182,7 @@
     xn = _rms(h_ref[...], g1[0:1, :])
     for cp in ck:
         cp.start()
-    _qkv_stage(me, xn, wbuf, cq, 0, sendA, recvA, sa, ra, qkv_ref)
+    _qkv_stage(True, me, xn, wbuf, cq, 0, sendA, recvA, sa, ra, qkv_ref)
     for cp in ck:
         cp.wait()
 
@@ -184,21 +195,24 @@
     wbuf, recvB, att, u, psend, pown, precv, chips, tot = sc[:9]
     wsem, sb, rb, s1, r1, s2, r2, s3, r3 = sc[9:18]
     dp, sp, c, me = _ids()
+    _hello(me)
     cm = _mlp_copies(l, dp, c, wo, w1, w2, wbuf, wsem)
-    ck = []
+    ck, cq = [], []
     if not last:
         sendA, recvA, sa, ra, ks = sc[18:]
         cq = _qkv_copies(l + 1, me, (wq, wk, wv), wbuf, wsem, 2, 24)
         ck = _cache_copies(l + 1, kc, vc, kb, vb, ks)
-    for cp in cm + ck:
-        cp.start()
-    _barrier(me)
-    cps = _exchange(me, lambda d: op_ref.at[2 * lax.rem(d, 4) + d // 4], recvB.at[me], sb, rb)
-    recvB[me] = op_ref[2 * sp + dp]
+    for cp in cm[:16]:
+        cp.start()
     h_ref[...] = hin[...]
     att[...] = jnp.zeros_like(att)
+    recvB[me] = op_ref[2 * sp + dp]
+    _barrier()
+    cps = _exchange(me, lambda d: op_ref.at[2 * lax.rem(d, 4) + d // 4], recvB.at[me], sb, rb)
     for cp in cps:
         cp.wait()
+    for cp in cm[16:]:
+        cp.start()
     for g in range(2):
         ms = [recvB[4 * g + i, 1][:, 0:1] for i in range(4)]
         m = functools.reduce(jnp.maximum, ms)
@@ -213,10 +227,11 @@
             for j in range(4):
                 att[2 * g + b:2 * g + b + 1, j * 128:(j + 1) * 128] = a[4 * b + j:4 * b + j + 1]
     av = att[...].astype(BF16)
+    for cp in cm[:8]:
+        cp.wait()
 
     def wo_block(t, q):
         n = 2 * t + q
-        cm[n].wait()
         return _dot(av, wbuf[n // 4, (n % 4) * 512:(n % 4) * 512 + 512, :])
 
     def bufs(i):
@@ -226,21 +241,23 @@
         return [s1.at[i], r1.at[i], s2.at[i], r2.at[i], s3.at[i], r3.at[i]]
 
     _allreduce(wo_block, dp, sp, c, me, bufs(0), sems(0), h_ref)
+    for cp in ck:
+        cp.start()
     xn = _rms(h_ref[...], g2[l:l + 1, :])
+    for cp in cm[8:16]:
+        cp.wait()
     for j in range(4):
-        cm[8 + 2 * j].wait()
         z = _dot(xn[:, :2048], wbuf[2 + 2 * j])
-        cm[9 + 2 * j].wait()
         z = z + _dot(xn[:, 2048:], wbuf[3 + 2 * j])
         u[:, j * NB:(j + 1) * NB] = _gelu(z).astype(BF16)
     uv = u[...]
-    if not last:
-        for cp in cq:
-            cp.start()
+    for cp in cm[16:]:
+        cp.wait()
+    for cp in cq:
+        cp.start()
 
     def w2_block(t, q):
         n = 2 * t + q
-        cm[16 + n].wait()
         return _dot(uv, wbuf[10 + n])
 
     _allreduce(w2_block, dp, sp, c, me, bufs(1), sems(1), h_ref)
@@ -249,7 +266,7 @@
         y_ref[...] = jnp.where(dp == 0, hv[0:2], hv[2:4]).astype(BF16)
     else:
         xn = _rms(h_ref[...], g1[l + 1:l + 2, :])
-        _qkv_stage(me, xn, wbuf, cq, 2, sendA, recvA, sa, ra, qkv_ref)
+        _qkv_stage(False, me, xn, wbuf, cq, 2, sendA, recvA, sa, ra, qkv_ref)
         for cp in ck:
             cp.wait()
 
@@ -259,7 +276,7 @@
         lensh, qkv, kin, vin, ko, vo, op_ref, kb, vb, *sc = refs
     else:
         lensh, qkv, kin, vin, _, _, ko, vo, op_ref, kb, vb, *sc = refs
-    lens, tr, s_ref, m_ref, l_ref, o_ref, ls, kos, vos = sc
+    lens, tr, q_ref, s_ref, m_ref, l_ref, o_ref, ls, kos, vos = sc
     nb, npos, nh, dh = kb.shape
     per = npos // CH
     n = nb * per
@@ -278,6 +295,11 @@
     m_ref[...] = jnp.full(m_ref.shape, -jnp.inf, F32)
     l_ref[...] = jnp.zeros_like(l_ref)
     o_ref[...] = jnp.zeros_like(o_ref)
+    z = jnp.zeros((nh, dh), BF16)
+    for b in range(nb):
+        q = tr[:, b, :].astype(BF16)
+        q_ref[b, 0:nh] = jnp.concatenate([q, z], axis=1)
+        q_ref[b, nh:2 * nh] = jnp.concatenate([z, q], axis=1)
     cl.wait()
     for b in range(nb):
         lp = lens[b] - 1 - base
@@ -287,41 +309,60 @@
             kb[b, lp] = tr[:, 2 + b, :].astype(BF16)
             vb[b, lp] = tr[:, 4 + b, :].astype(BF16)
 
-    row = lax.broadcasted_iota(jnp.int32, (nh, CH * nh), 0)
-    col = lax.broadcasted_iota(jnp.int32, (nh, CH * nh), 1)
-    same = lax.rem(col, nh) == row
-
-    def kstep(i, _):
-        b = i // per
-        p0 = pl.multiple_of(lax.rem(i, per) * CH, CH)
-        q = tr[:, b, :].astype(BF16)
-        kk = kb[b, pl.ds(p0, CH)].reshape(CH * nh, dh)
-        s = lax.dot_general(q, kk, (((1,), (1,)), ((), ())), preferred_element_type=F32) * dh ** -0.5
-        lim = (lens[b] - base - p0) * nh
-        s = jnp.where(same & (col < lim), s, -jnp.inf)
-        s_ref[i] = s
-        m_ref[b] = jnp.maximum(m_ref[b], jnp.max(s, axis=1, keepdims=True))
+    hc = CH * nh // 2
+    row = lax.broadcasted_iota(jnp.int32, (2 * nh, hc), 0)
+    col = lax.broadcasted_iota(jnp.int32, (2 * nh, hc), 1)
+    same = lax.rem(col, nh) == lax.rem(row, nh)
+    at = col + (row // nh) * hc
+
+    def pair(buf, b, p0):
+        return jnp.concatenate([buf[b, pl.ds(p0, CH // 2)].reshape(hc, dh),
+                                buf[b, pl.ds(p0 + CH // 2, CH // 2)].reshape(hc, dh)], axis=1)
+
+    for i in range(n):
         wr(ko, kb, kos, i).start()
         wr(vo, vb, vos, i).start()
+
+    def kstep(t, _):
+        b = t * 4 // per
+        for j in range(4):
+            i = t * 4 + j
+            p0 = pl.multiple_of(lax.rem(i, per) * CH, CH)
+            s = lax.dot_general(q_ref[b], pair(kb, b, p0), (((1,), (1,)), ((), ())),
+                                preferred_element_type=F32) * dh ** -0.5
+            lim = (lens[b] - base - p0) * nh
+            s = jnp.where(same & (at < lim), s, -jnp.inf)
+            s_ref[i] = s
+            m_ref[b] = jnp.maximum(m_ref[b], jnp.max(s, axis=1, keepdims=True))
         return 0
 
-    def vstep(i, _):
-        b = i // per
-        p0 = pl.multiple_of(lax.rem(i, per) * CH, CH)
+    def vstep(t, _):
+        b = t * 4 // per
         m = m_ref[b][:, 0:1]
+        lt, ot = l_ref[b], o_ref[b]
+        for j in range(4):
+            i = t * 4 + j
+            p0 = pl.multiple_of(lax.rem(i, per) * CH, CH)
+            p = jnp.exp(s_ref[i] - m)
+            lt = lt + jnp.sum(p, axis=1, keepdims=True)
+            ot = ot + _dot(p.astype(BF16), pair(vb, b, p0))
+        l_ref[b] = lt
+        o_ref[b] = ot
+        return 0
+
+    lax.fori_loop(0, n // 4, kstep, 0)
+    mt = []
+    for b in range(nb):
+        m = jnp.maximum(m_ref[b, 0:nh], m_ref[b, nh:2 * nh])
+        mt.append(m)
         m = jnp.where(m == -jnp.inf, 0.0, m)
-        p = jnp.exp(s_ref[i] - m)
-        l_ref[b] += jnp.sum(p, axis=1, keepdims=True)
-        vv = vb[b, pl.ds(p0, CH)].reshape(CH * nh, dh)
-        o_ref[b] += _dot(p.astype(BF16), vv)
-        return 0
-
-    lax.fori_loop(0, n, kstep, 0)
-    lax.fori_loop(0, n, vstep, 0)
+        m_ref[b, 0:nh] = m
+        m_ref[b, nh:2 * nh] = m
+    lax.fori_loop(0, n // 4, vstep, 0)
     lane = lax.broadcasted_iota(jnp.int32, (nh, dh), 1)
     for b in range(nb):
-        ov = o_ref[b]
-        ml = jnp.where(lane < 64, m_ref[b], l_ref[b])
+        ov = o_ref[b, 0:nh, 0:dh] + o_ref[b, nh:2 * nh, dh:2 * dh]
+        ml = jnp.where(lane < 64, mt[b], l_ref[b, 0:nh] + l_ref[b, nh:2 * nh])
         for r in range(8):
             op_ref[r, 0, b * 4:b * 4 + 4, :] = ov[4 * r:4 * r + 4]
             op_ref[r, 1, b * 4:b * 4 + 4, :] = ml[4 * r:4 * r + 4]
@@ -348,10 +389,10 @@
 
         h, qkv, kb, vb = pl.pallas_call(
             _first, out_shape=(h_sh, qkv_sh, c_vm, c_vm),
-            in_specs=[VM, ANY, ANY, ANY, VM, ANY, ANY], out_specs=(VM,) * 4,
-            scratch_shapes=[V((6, 2048, NB), BF16), V((2, d), BF16), *qkv_sc,
-                            DMA((6,)), DMA, DMA, DMA((8,)), DMA((8,)), DMA((2, nb))],
-            compiler_params=cparams(0, 16), name='first')(*(vm(x) + hbm(wq, wk, wv) + vm(g1) + hbm(kc, vc)))
+            in_specs=[ANY] * 7, out_specs=(VM,) * 4,
+            scratch_shapes=[V((6, 2048, NB), BF16), V((2, d), BF16), V((2, d), BF16), V((nl, d), BF16), *qkv_sc,
+                            DMA((6,)), DMA, DMA, DMA((8,)), DMA((8,)), DMA((2,)), DMA((2, nb))],
+            compiler_params=cparams(0, 16), name='first')(*hbm(x, wq, wk, wv, g1, kc, vc))
 
         def attn(l, qkv, kb, vb, ko, vo):
             n = nb * npos // CH
@@ -365,8 +406,9 @@
                 out_shape=(c_sh, c_sh, V((8, 2, 8, dh), F32), c_vm, c_vm),
                 in_specs=[ANY, VM, VM, VM] + ([] if l == 0 else [ANY, ANY]),
                 out_specs=(ANY, ANY, VM, VM, VM),
-                scratch_shapes=[pltpu.SMEM((nb,), jnp.int32), V((nh, 8, dh), F32), V((n, nh, CH * nh), F32),
-                                V((nb, nh, dh), F32), V((nb, nh, dh), F32), V((nb, nh, dh), F32),
+                scratch_shapes=[pltpu.SMEM((nb,), jnp.int32), V((nh, 8, dh), F32), V((nb, 2 * nh, 2 * dh), BF16),
+                                V((n, 2 * nh, CH * nh // 2), F32), V((nb, 2 * nh, dh), F32),
+                                V((nb, 2 * nh, dh), F32), V((nb, 2 * nh, 2 * dh), F32),
                                 DMA, DMA((n,)), DMA((n,))],
                 input_output_aliases=al,
                 compiler_params=pltpu.CompilerParams(vmem_limit_bytes=14 * 2 ** 20), name='attn')(*args)[:3]

time: 85.3 us -> 76.7 us (0.90)
  Pallas kernels: 82.2 us -> 75.1 us
  local copies, waits for them, and re-layouts: 2.05 us -> 0.62 us
    pallas_call x2, Pallas kernels: 52.4 us -> 48.6 us  [layer(): pl.pallas_call(functools.partial(_layer, l, last), out_shape=outs, in_spe...]
    pallas_call x2, Pallas kernels: 17.1 us -> 13.7 us  [attn(): pl.pallas_call(functools.partial(_attn, l), out_shape=(c_sh, c_sh, V((8,...]
    unnamed x9 -> x5, local copies, waits for them, and re-layouts: 2.05 us -> 0.62 us
where the time goes in v4:
time: 76.7 us; the launch traced here: 76.4 us
  Pallas kernels  75.1 us (98%)
    pallas_call x2, Pallas kernels, layer(): pl.pallas_call(functools.partial(_layer, l, last), out_shape=outs, in_spe...  48.6 us
    pallas_call x2, Pallas kernels, attn(): pl.pallas_call(functools.partial(_attn, l), out_shape=(c_sh, c_sh, V((8,...  13.7 us
    pallas_call x1, Pallas kernels, local(): pl.pallas_call(_first, out_shape=(h_sh, qkv_sh, c_vm, c_vm), in_specs=[AN...  12.8 us

profile of v4, /device:TPU:0, one launch (start us, length us, event | category | flops | bytes accessed | tf_op | source)
XLA Modules:
  0.0 76.4 jit_solution(8518958108116936690)
XLA Ops:
  0.6 12.8 %first.1 = (f32[8,4096]{1,0:T(8,128)S(1)}, bf16[8,8,512]{2,1,0:T(8,128)(2,1)S(1)}, bf16[2,512,32,128]{3,2,1,0:T(8,128)(2,1)S(1)}, bf16[2,512,32,128]{3,2,1,0:T(8,128)(2,1)S(1)}) custom-call(bf16[2,4096]{1,0:T(2,128)(2,1)} %x.1, bf16[2,4096,4096]{2,1,0:T(8,128)(2,1)} %refs_6_.1, bf16[2,4096,4096]{2,1,0:T(8,128)(2,1)} %refs_7_.1, ...), custom_call_target="tpu_custom_call" | custom-call | tf_op jit(solution)/shard_map/first/pallas_call | solution.py:390
  13.4 0.0 copy-start
  13.4 0.0 copy-start.1
  13.5 6.8 %attn.2 = (bf16[2,2,512,32,128]{4,3,2,1,0:T(8,128)(2,1)}, bf16[2,2,512,32,128]{4,3,2,1,0:T(8,128)(2,1)}, f32[8,2,8,128]{3,2,1,0:T(8,128)S(1)}, bf16[2,512,32,128...) custom-call(s32[2]{0:T(128)} %refs_0_.3, ...), custom_call_target="tpu_custom_call", output_to_operand_aliasing={{3}: (2, {}), {4}: (3, {})} | custom-call | tf_op jit(solution)/shard_map/attn/pallas_call | solution.py:404
  20.3 0.0 copy-done
  20.3 0.0 copy-done.1
  20.3 27.4 %layer.2 = (f32[8,4096]{1,0:T(8,128)S(1)}, bf16[8,8,512]{2,1,0:T(8,128)(2,1)S(1)}, bf16[2,512,32,128]{3,2,1,0:T(8,128)(2,1)S(1)}, bf16[2,512,32,128]{3,2,1,0:T(8,128)(2,1)S(1)}) custom-call(f32[8,2,8,128]{3,2,1,0:T(8,128)S(1)} %get-tuple-element.20.refs_0_, f32[8,4096]{1,0:T(8,128)S(1)} %get-tuple-element.21.refs_1_, bf16[2,1024,4096]{2,1,0:T(8,128)(2,1)} %refs_2_.3, ...), custom_call_target="tpu_custom_call" | custom-call | tf_op jit(solution)/shard_map/layer/pallas_call | solution.py:433
  47.8 6.9 %attn.3 = (bf16[2,2,512,32,128]{4,3,2,1,0:T(8,128)(2,1)}, bf16[2,2,512,32,128]{4,3,2,1,0:T(8,128)(2,1)}, f32[8,2,8,128]{3,2,1,0:T(8,128)S(1)}, bf16[2,512,32,128...) custom-call(s32[2]{0:T(128)} %refs_0_.3, ...), custom_call_target="tpu_custom_call", output_to_operand_aliasing={{3}: (2, {}), {4}: (3, {}), {0}: (4, {}), {1}: (5, {})} | custom-call | tf_op jit(solution)/shard_map/attn/pallas_call | solution.py:404
  54.6 21.1 %layer.3 = bf16[2,4096]{1,0:T(2,128)(2,1)S(1)} custom-call(f32[8,2,8,128]{3,2,1,0:T(8,128)S(1)} %get-tuple-element.27.refs_0_, f32[8,4096]{1,0:T(8,128)S(1)} %get-tuple-element.28.refs_1_, bf16[2,1024,4096]{2,1,0:T(8,128)(2,1)} %refs_2_.3, bf16[2,4096,4096]{2,1,0:T(8,128)(2,1)} %refs_3_.3, bf16[2,4096,4096]{2,1,0:T(8,128)(2,1)} %refs_4_.3, ...), custom_call_target="tpu_custom_call" | custom-call | tf_op jit(solution)/shard_map/layer/pallas_call | solution.py:433
  75.8 0.6 copy.28
Async XLA Ops:
  13.4 6.9 %copy-start = (bf16[2,4096]{1,0:T(2,128)(2,1)S(1)}, bf16[2,4096]{1,0:T(2,128)(2,1)}, u32[]{:S(2)}) copy-start(bf16[2,4096]{1,0:T(2,128)(2,1)} %refs_9_.1) | copy-start | bytes 49156
  13.4 6.8 %copy-start.1 = (bf16[2,4096]{1,0:T(2,128)(2,1)S(1)}, bf16[2,4096]{1,0:T(2,128)(2,1)}, u32[]{:S(2)}) copy-start(bf16[2,4096]{1,0:T(2,128)(2,1)} %refs_5_.3) | copy-start | bytes 49156

commit v5 on v4

--- a/solution.py
+++ b/solution.py
@@ -8,6 +8,7 @@
 from jax.sharding import PartitionSpec as P
 
 EPS = 1e-6
+LOG2E = 1.4426950408889634
 MESH = pl.DeviceIdType.MESH
 VM = pl.BlockSpec(memory_space=pltpu.VMEM)
 ANY = pl.BlockSpec(memory_space=pltpu.HBM)
@@ -47,14 +48,15 @@
     pl.semaphore_wait(pltpu.get_barrier_semaphore(), 7)
 
 
-def _exchange(me, src, dst, ssem, rsem):
+def _exchange(dp, sp, c, src, dst, ssem, rsem):
+    x = sp // 2
+    devs = [(1 - dp, (1 - x) * 2 + 1 - c), (1 - dp, (1 - x) * 2 + c), (1 - dp, x * 2 + 1 - c), (1 - dp, sp),
+            (dp, (1 - x) * 2 + 1 - c), (dp, (1 - x) * 2 + c), (dp, sp + 1 - 2 * c)]
     out = []
-    for k in range(1, 8):
-        d = lax.rem(me + k, 8)
-        c = pltpu.make_async_remote_copy(src(d), dst, ssem.at[k], rsem.at[k],
-                                         device_id=(d // 4, lax.rem(d, 4)), device_id_type=MESH)
-        c.start()
-        out.append(c)
+    for k, dev in enumerate(devs):
+        cp = pltpu.make_async_remote_copy(src(*dev), dst, ssem.at[k], rsem.at[k], device_id=dev, device_id_type=MESH)
+        cp.start()
+        out.append(cp)
     return out
 
 
@@ -99,41 +101,51 @@
     return out
 
 
-def _allreduce(block, dp, sp, c, me, buf, sems, h_ref):
+def _allreduce(block, dp, sp, c, buf, sems, h_ref):
     psend, pown, precv, chips, tot = buf
     s1, r1, s2, r2, s3, r3 = sems
+    x = sp // 2
     partner = (dp, sp + 1 - 2 * c)
+    chip = dp * 2 + x
+    devs = ((1 - dp, (1 - x) * 2 + c), (1 - dp, sp), (dp, (1 - x) * 2 + c))
+
+    def both(t):
+        return jnp.concatenate([block(t, 0)[0:4], block(t, 1)[0:4]], axis=0)
+
+    def copy(src, dst, ss, rs, dev):
+        return pltpu.make_async_remote_copy(src, dst, ss, rs, device_id=dev, device_id_type=MESH)
+
+    one = [copy(psend.at[t], precv.at[t], s1.at[t], r1.at[t], partner) for t in range(2)]
+    two = [[copy(chips.at[chip, t], chips.at[chip, t], s2.at[t, k], r2.at[t, k], dev)
+            for k, dev in enumerate(devs)] for t in range(2)]
+    three = [copy(tot.at[c, t], tot.at[c, t], s3.at[t], r3.at[t], partner) for t in range(2)]
     for t in range(2):
-        v = jnp.concatenate([block(t, 0)[0:4], block(t, 1)[0:4]], axis=0)
-        psend[:, t * NB:(t + 1) * NB] = v
-    one = pltpu.make_async_remote_copy(psend, precv, s1, r1, device_id=partner, device_id_type=MESH)
-    one.start()
+        psend[t] = both(t)
+        one[t].start()
     for t in range(2):
-        v = jnp.concatenate([block(t + 2, 0)[0:4], block(t + 2, 1)[0:4]], axis=0)
-        pown[:, t * NB:(t + 1) * NB] = v
-    one.wait()
-    chip = dp * 2 + sp // 2
-    chips[chip] = pown[...] + precv[...]
-    two = []
-    for k in range(1, 4):
-        d = lax.rem(chip + k, 4)
-        cp = pltpu.make_async_remote_copy(chips.at[chip], chips.at[chip], s2.at[k], r2.at[k],
-                                          device_id=(d // 2, lax.rem(d, 2) * 2 + c), device_id_type=MESH)
-        cp.start()
-        two.append(cp)
-    for cp in two:
-        cp.wait()
-    tot[c] = ((chips[0] + chips[1]) + chips[2]) + chips[3]
-    three = pltpu.make_async_remote_copy(tot.at[c], tot.at[c], s3, r3, device_id=partner, device_id_type=MESH)
-    three.start()
-    three.wait()
-    for half in range(2):
+        pown[t] = both(2 + t)
+        one[t].wait()
+        chips[chip, t] = pown[t] + precv[t]
+        for cp in two[t]:
+            cp.start()
+    for t in range(2):
+        for cp in two[t]:
+            cp.wait()
+        tot[c, t] = ((chips[0, t] + chips[1, t]) + chips[2, t]) + chips[3, t]
+        three[t].start()
+    def add(half, t):
         for q in range(2):
-            lo = half * 2048 + q * 1024
-            h_ref[0:4, lo:lo + 1024] += tot[half, q * 4:q * 4 + 4, :]
-
-
-def _qkv_stage(chase, me, xn, wbuf, copies, slot, sendA, recvA, ssem, rsem, qkv_ref):
+            cols = pl.ds(pl.multiple_of(half * 2048 + q * 1024 + t * NB, NB), NB)
+            h_ref[0:4, cols] += tot[half, t, q * 4:q * 4 + 4, :]
+
+    for t in range(2):
+        add(c, t)
+    for t in range(2):
+        three[t].wait()
+        add(1 - c, t)
+
+
+def _qkv_stage(chase, dp, sp, c, me, xn, wbuf, copies, slot, sendA, recvA, ssem, rsem, qkv_ref):
     res = []
     step = 2 if chase else 6
     for i in range(3):
@@ -146,8 +158,8 @@
     for g in range(2):
         rows = [r[2 * g:2 * g + 2] for r in res] + [jnp.zeros((2, NB), F32)]
         sendA[g] = jnp.concatenate(rows, axis=0).astype(BF16)
-    cps = _exchange(me, lambda d: sendA.at[d // 4], recvA.at[me], ssem, rsem)
-    recvA[me] = sendA[me // 4]
+    cps = _exchange(dp, sp, c, lambda p, s: sendA.at[p], recvA.at[me], ssem, rsem)
+    recvA[me] = sendA[dp]
     for cp in cps:
         cp.wait()
     qkv_ref[...] = recvA[...]
@@ -165,11 +177,11 @@
     ck = _cache_copies(0, kc, vc, kb, vb, ks)
     _hello(me)
     cs = [pltpu.make_async_copy(x, xm, gs.at[0]), pltpu.make_async_copy(g1h, g1, gs.at[1])]
+    for cp in cs + cq[:1]:
+        cp.start()
     for cp in cs:
-        cp.start()
-    for cp in cs:
-        cp.wait()
-    for cp in cq:
+        cp.wait()
+    for cp in cq[1:]:
         cp.start()
     _barrier()
     ex = pltpu.make_async_remote_copy(xm, xo, xs, xr, device_id=(1 - dp, sp), device_id_type=MESH)
@@ -182,7 +194,7 @@
     xn = _rms(h_ref[...], g1[0:1, :])
     for cp in ck:
         cp.start()
-    _qkv_stage(True, me, xn, wbuf, cq, 0, sendA, recvA, sa, ra, qkv_ref)
+    _qkv_stage(True, dp, sp, c, me, xn, wbuf, cq, 0, sendA, recvA, sa, ra, qkv_ref)
     for cp in ck:
         cp.wait()
 
@@ -208,7 +220,7 @@
     att[...] = jnp.zeros_like(att)
     recvB[me] = op_ref[2 * sp + dp]
     _barrier()
-    cps = _exchange(me, lambda d: op_ref.at[2 * lax.rem(d, 4) + d // 4], recvB.at[me], sb, rb)
+    cps = _exchange(dp, sp, c, lambda p, s: op_ref.at[2 * s + p], recvB.at[me], sb, rb)
     for cp in cps:
         cp.wait()
     for cp in cm[16:]:
@@ -219,7 +231,7 @@
         o = jnp.zeros((8, 128), F32)
         den = jnp.zeros((8, 1), F32)
         for i in range(4):
-            e = jnp.exp(ms[i] - m)
+            e = jnp.exp2(ms[i] - m)
             o = o + recvB[4 * g + i, 0] * e
             den = den + recvB[4 * g + i, 1][:, 64:65] * e
         a = o / den
@@ -240,7 +252,7 @@
     def sems(i):
         return [s1.at[i], r1.at[i], s2.at[i], r2.at[i], s3.at[i], r3.at[i]]
 
-    _allreduce(wo_block, dp, sp, c, me, bufs(0), sems(0), h_ref)
+    _allreduce(wo_block, dp, sp, c, bufs(0), sems(0), h_ref)
     for cp in ck:
         cp.start()
     xn = _rms(h_ref[...], g2[l:l + 1, :])
@@ -260,13 +272,13 @@
         n = 2 * t + q
         return _dot(uv, wbuf[10 + n])
 
-    _allreduce(w2_block, dp, sp, c, me, bufs(1), sems(1), h_ref)
+    _allreduce(w2_block, dp, sp, c, bufs(1), sems(1), h_ref)
     if last:
         hv = h_ref[...]
         y_ref[...] = jnp.where(dp == 0, hv[0:2], hv[2:4]).astype(BF16)
     else:
         xn = _rms(h_ref[...], g1[l + 1:l + 2, :])
-        _qkv_stage(False, me, xn, wbuf, cq, 2, sendA, recvA, sa, ra, qkv_ref)
+        _qkv_stage(False, dp, sp, c, me, xn, wbuf, cq, 2, sendA, recvA, sa, ra, qkv_ref)
         for cp in ck:
             cp.wait()
 
@@ -276,13 +288,13 @@
         lensh, qkv, kin, vin, ko, vo, op_ref, kb, vb, *sc = refs
     else:
         lensh, qkv, kin, vin, _, _, ko, vo, op_ref, kb, vb, *sc = refs
-    lens, tr, q_ref, s_ref, m_ref, l_ref, o_ref, ls, kos, vos = sc
+    tr, q_ref, s_ref, m_ref, l_ref, o_ref, kos, vos = sc
     nb, npos, nh, dh = kb.shape
     per = npos // CH
     n = nb * per
     base = lax.axis_index('sp') * npos
-    cl = pltpu.make_async_copy(lensh, lens, ls)
-    cl.start()
+    lv = lensh[...]
+    lens = [jnp.max(lv[:, b:b + 1]) for b in range(nb)]
 
     def wr(dst, buf, sem, i):
         b, p = i // per, pl.multiple_of(lax.rem(i, per) * CH, CH)
@@ -300,7 +312,6 @@
         q = tr[:, b, :].astype(BF16)
         q_ref[b, 0:nh] = jnp.concatenate([q, z], axis=1)
         q_ref[b, nh:2 * nh] = jnp.concatenate([z, q], axis=1)
-    cl.wait()
     for b in range(nb):
         lp = lens[b] - 1 - base
 
@@ -310,10 +321,25 @@
             vb[b, lp] = tr[:, 4 + b, :].astype(BF16)
 
     hc = CH * nh // 2
-    row = lax.broadcasted_iota(jnp.int32, (2 * nh, hc), 0)
-    col = lax.broadcasted_iota(jnp.int32, (2 * nh, hc), 1)
-    same = lax.rem(col, nh) == lax.rem(row, nh)
-    at = col + (row // nh) * hc
+    sl = lax.broadcasted_iota(jnp.int32, (8, dh), 0)
+    ln = lax.broadcasted_iota(jnp.int32, (8, dh), 1)
+    tile = lambda v: jnp.concatenate([v] * (hc // dh), axis=1)
+    diag = tile(lax.rem(ln, nh) - sl)
+    group = tile(lax.rem(ln, nh) // 8)
+    col = lax.broadcasted_iota(jnp.int32, (8, hc), 1)
+    ng = nh // 8
+    sc = dh ** -0.5 * LOG2E
+
+    def heads(v, op):
+        k = nh
+        while k < dh:
+            v = op(v, pltpu.roll(v, k, 1))
+            k *= 2
+        return v
+
+    def column(v, fill, op):
+        return jnp.concatenate([op(jnp.where(ln == sl + 8 * r, v, fill), axis=1, keepdims=True)
+                                for r in range(ng)], axis=0)
 
     def pair(buf, b, p0):
         return jnp.concatenate([buf[b, pl.ds(p0, CH // 2)].reshape(hc, dh),
@@ -323,46 +349,48 @@
         wr(ko, kb, kos, i).start()
         wr(vo, vb, vos, i).start()
 
-    def kstep(t, _):
-        b = t * 4 // per
-        for j in range(4):
-            i = t * 4 + j
-            p0 = pl.multiple_of(lax.rem(i, per) * CH, CH)
-            s = lax.dot_general(q_ref[b], pair(kb, b, p0), (((1,), (1,)), ((), ())),
-                                preferred_element_type=F32) * dh ** -0.5
-            lim = (lens[b] - base - p0) * nh
-            s = jnp.where(same & (at < lim), s, -jnp.inf)
-            s_ref[i] = s
-            m_ref[b] = jnp.maximum(m_ref[b], jnp.max(s, axis=1, keepdims=True))
+    def pick(b):
+        return functools.reduce(lambda v, i: jnp.where(b == i, lens[i], v), range(1, nb), lens[0])
+
+    def kstep(b, _):
+        m = m_ref[b]
+        for j in range(per):
+            s = lax.dot_general(q_ref[b], pair(kb, b, j * CH), (((1,), (1,)), ((), ())),
+                                preferred_element_type=F32)
+            lim = (pick(b) - base - j * CH) * nh
+            for half in range(2):
+                v = functools.reduce(jnp.maximum, [
+                    jnp.where(diag == 8 * r, s[half * nh + 8 * r:half * nh + 8 * r + 8], -jnp.inf) for r in range(ng)])
+                v = jnp.where(col < lim - half * hc, v, -jnp.inf)
+                s_ref[b * per + j, half] = v
+                for k in range(0, hc, dh):
+                    m = jnp.maximum(m, v[:, k:k + dh])
+        m_ref[b] = heads(m, jnp.maximum)
         return 0
 
-    def vstep(t, _):
-        b = t * 4 // per
-        m = m_ref[b][:, 0:1]
+    def vstep(b, _):
+        m = m_ref[b]
+        m = tile(jnp.where(m == -jnp.inf, 0.0, m))
         lt, ot = l_ref[b], o_ref[b]
-        for j in range(4):
-            i = t * 4 + j
-            p0 = pl.multiple_of(lax.rem(i, per) * CH, CH)
-            p = jnp.exp(s_ref[i] - m)
-            lt = lt + jnp.sum(p, axis=1, keepdims=True)
-            ot = ot + _dot(p.astype(BF16), pair(vb, b, p0))
-        l_ref[b] = lt
+        for j in range(per):
+            rows = []
+            for half in range(2):
+                p = jnp.exp2((s_ref[b * per + j, half] - m) * sc)
+                for k in range(0, hc, dh):
+                    lt = lt + p[:, k:k + dh]
+                rows += [jnp.where(group == r, p, 0.0) for r in range(ng)]
+            ot = ot + _dot(jnp.concatenate(rows, axis=0).astype(BF16), pair(vb, b, j * CH))
+        l_ref[b] = heads(lt, jnp.add)
         o_ref[b] = ot
         return 0
 
-    lax.fori_loop(0, n // 4, kstep, 0)
-    mt = []
-    for b in range(nb):
-        m = jnp.maximum(m_ref[b, 0:nh], m_ref[b, nh:2 * nh])
-        mt.append(m)
-        m = jnp.where(m == -jnp.inf, 0.0, m)
-        m_ref[b, 0:nh] = m
-        m_ref[b, nh:2 * nh] = m
-    lax.fori_loop(0, n // 4, vstep, 0)
+    lax.fori_loop(0, nb, kstep, 0)
+    lax.fori_loop(0, nb, vstep, 0)
     lane = lax.broadcasted_iota(jnp.int32, (nh, dh), 1)
     for b in range(nb):
         ov = o_ref[b, 0:nh, 0:dh] + o_ref[b, nh:2 * nh, dh:2 * dh]
-        ml = jnp.where(lane < 64, mt[b], l_ref[b, 0:nh] + l_ref[b, nh:2 * nh])
+        mc = column(m_ref[b], -jnp.inf, jnp.max) * sc
+        ml = jnp.where(lane < 64, mc, column(l_ref[b], 0.0, jnp.sum))
         for r in range(8):
             op_ref[r, 0, b * 4:b * 4 + 4, :] = ov[4 * r:4 * r + 4]
             op_ref[r, 1, b * 4:b * 4 + 4, :] = ml[4 * r:4 * r + 4]
@@ -397,29 +425,29 @@
         def attn(l, qkv, kb, vb, ko, vo):
             n = nb * npos // CH
             c_sh = jax.ShapeDtypeStruct(kc.shape, kc.dtype)
-            args = hbm(lens) + vm(qkv, kb, vb) + ([] if l == 0 else hbm(ko, vo))
+            args = vm(lens.reshape(1, nb), qkv, kb, vb) + ([] if l == 0 else hbm(ko, vo))
             al = {2: 3, 3: 4}
             if l > 0:
                 al.update({4: 0, 5: 1})
             return pl.pallas_call(
                 functools.partial(_attn, l),
                 out_shape=(c_sh, c_sh, V((8, 2, 8, dh), F32), c_vm, c_vm),
-                in_specs=[ANY, VM, VM, VM] + ([] if l == 0 else [ANY, ANY]),
+                in_specs=[VM, VM, VM, VM] + ([] if l == 0 else [ANY, ANY]),
                 out_specs=(ANY, ANY, VM, VM, VM),
-                scratch_shapes=[pltpu.SMEM((nb,), jnp.int32), V((nh, 8, dh), F32), V((nb, 2 * nh, 2 * dh), BF16),
-                                V((n, 2 * nh, CH * nh // 2), F32), V((nb, 2 * nh, dh), F32),
-                                V((nb, 2 * nh, dh), F32), V((nb, 2 * nh, 2 * dh), F32),
-                                DMA, DMA((n,)), DMA((n,))],
+                scratch_shapes=[V((nh, 8, dh), F32), V((nb, 2 * nh, 2 * dh), BF16),
+                                V((n, 2, 8, CH * nh // 2), F32), V((nb, 8, dh), F32),
+                                V((nb, 8, dh), F32), V((nb, 2 * nh, 2 * dh), F32),
+                                DMA((n,)), DMA((n,))],
                 input_output_aliases=al,
                 compiler_params=pltpu.CompilerParams(vmem_limit_bytes=14 * 2 ** 20), name='attn')(*args)[:3]
 
         def layer(l, op, h, last):
             sc = [V((18, 2048, NB), BF16), V((8, 2, 8, dh), F32),
                   V((8, 512), F32), V((8, 2048), BF16),
-                  V((2, 8, 1024), F32), V((2, 8, 1024), F32), V((2, 8, 1024), F32),
-                  V((2, 4, 8, 1024), F32), V((2, 2, 8, 1024), F32),
+                  V((2, 2, 8, NB), F32), V((2, 2, 8, NB), F32), V((2, 2, 8, NB), F32),
+                  V((2, 4, 2, 8, NB), F32), V((2, 2, 2, 8, NB), F32),
                   DMA((30,)), DMA((8,)), DMA((8,)),
-                  DMA((2,)), DMA((2,)), DMA((2, 4)), DMA((2, 4)), DMA((2,)), DMA((2,))]
+                  DMA((2, 2)), DMA((2, 2)), DMA((2, 2, 3)), DMA((2, 2, 3)), DMA((2, 2)), DMA((2, 2))]
             args = vm(op, h) + hbm(wo, w1, w2) + vm(g2)
             specs = [VM, VM, ANY, ANY, ANY, VM]
             if last:

time: 76.7 us -> 74.4 us (0.970)
  Pallas kernels: 75.1 us -> 72.9 us
    pallas_call x2, Pallas kernels: 13.7 us -> 12.4 us  [attn(): pl.pallas_call(functools.partial(_attn, l), out_shape=(c_sh, c_sh, V((8,...]
    pallas_call x2, Pallas kernels: 48.6 us -> 47.7 us  [layer(): pl.pallas_call(functools.partial(_layer, l, last), out_shape=outs, in_spe...]
where the time goes in v5:
time: 74.4 us; the launch traced here: 74.3 us
  Pallas kernels  72.9 us (98%)
    pallas_call x2, Pallas kernels, layer(): pl.pallas_call(functools.partial(_layer, l, last), out_shape=outs, in_spe...  47.7 us
    pallas_call x1, Pallas kernels, local(): pl.pallas_call(_first, out_shape=(h_sh, qkv_sh, c_vm, c_vm), in_specs=[AN...  12.8 us
    pallas_call x2, Pallas kernels, attn(): pl.pallas_call(functools.partial(_attn, l), out_shape=(c_sh, c_sh, V((8,...  12.4 us

profile of v5, /device:TPU:0, one launch (start us, length us, event | category | flops | bytes accessed | tf_op | source)
XLA Modules:
  0.0 74.3 jit_solution(13913434250223427161)
XLA Ops:
  0.6 0.0 copy-start.2
  0.6 12.8 %first.1 = (f32[8,4096]{1,0:T(8,128)S(1)}, bf16[8,8,512]{2,1,0:T(8,128)(2,1)S(1)}, bf16[2,512,32,128]{3,2,1,0:T(8,128)(2,1)S(1)}, bf16[2,512,32,128]{3,2,1,0:T(8,128)(2,1)S(1)}) custom-call(bf16[2,4096]{1,0:T(2,128)(2,1)} %x.1, bf16[2,4096,4096]{2,1,0:T(8,128)(2,1)} %refs_6_.1, bf16[2,4096,4096]{2,1,0:T(8,128)(2,1)} %refs_7_.1, ...), custom_call_target="tpu_custom_call" | custom-call | tf_op jit(solution)/shard_map/first/pallas_call | solution.py:418
  13.4 0.0 copy-start
  13.5 0.0 copy-start.1
  13.5 0.0 copy-done.2
  13.5 6.1 %attn.2 = (bf16[2,2,512,32,128]{4,3,2,1,0:T(8,128)(2,1)}, bf16[2,2,512,32,128]{4,3,2,1,0:T(8,128)(2,1)}, f32[8,2,8,128]{3,2,1,0:T(8,128)S(1)}, bf16[2,512,32,128...) custom-call(s32[1,2]{1,0:T(1,128)S(1)} %bitcast.1, ...), custom_call_target="tpu_custom_call", output_to_operand_aliasing={{3}: (2, {}), {4}: (3, {})} | custom-call | tf_op jit(solution)/shard_map/attn/pallas_call | solution.py:432
  19.6 0.0 copy-done
  19.6 0.0 copy-done.1
  19.6 27.0 %layer.2 = (f32[8,4096]{1,0:T(8,128)S(1)}, bf16[8,8,512]{2,1,0:T(8,128)(2,1)S(1)}, bf16[2,512,32,128]{3,2,1,0:T(8,128)(2,1)S(1)}, bf16[2,512,32,128]{3,2,1,0:T(8,128)(2,1)S(1)}) custom-call(f32[8,2,8,128]{3,2,1,0:T(8,128)S(1)} %get-tuple-element.20.refs_0_, f32[8,4096]{1,0:T(8,128)S(1)} %get-tuple-element.21.refs_1_, bf16[2,1024,4096]{2,1,0:T(8,128)(2,1)} %refs_2_.3, ...), custom_call_target="tpu_custom_call" | custom-call | tf_op jit(solution)/shard_map/layer/pallas_call | solution.py:461
  46.6 6.3 %attn.3 = (bf16[2,2,512,32,128]{4,3,2,1,0:T(8,128)(2,1)}, bf16[2,2,512,32,128]{4,3,2,1,0:T(8,128)(2,1)}, f32[8,2,8,128]{3,2,1,0:T(8,128)S(1)}, bf16[2,512,32,128...) custom-call(s32[1,2]{1,0:T(1,128)S(1)} %bitcast.2, ...), custom_call_target="tpu_custom_call", output_to_operand_aliasing={{3}: (2, {}), {4}: (3, {}), {0}: (4, {}), {1}: (5, {})} | custom-call | tf_op jit(solution)/shard_map/attn/pallas_call | solution.py:432
  52.9 20.7 %layer.3 = bf16[2,4096]{1,0:T(2,128)(2,1)S(1)} custom-call(f32[8,2,8,128]{3,2,1,0:T(8,128)S(1)} %get-tuple-element.27.refs_0_, f32[8,4096]{1,0:T(8,128)S(1)} %get-tuple-element.28.refs_1_, bf16[2,1024,4096]{2,1,0:T(8,128)(2,1)} %refs_2_.3, bf16[2,4096,4096]{2,1,0:T(8,128)(2,1)} %refs_3_.3, bf16[2,4096,4096]{2,1,0:T(8,128)(2,1)} %refs_4_.3, ...), custom_call_target="tpu_custom_call" | custom-call | tf_op jit(solution)/shard_map/layer/pallas_call | solution.py:461
  73.7 0.6 copy.28
Async XLA Ops:
  0.6 12.8 %copy-start.2 = (s32[2]{0:T(128)S(1)}, s32[2]{0:T(128)}, u32[]{:S(2)}) copy-start(s32[2]{0:T(128)} %param.13) | copy-start | bytes 28
  13.4 6.1 %copy-start = (bf16[2,4096]{1,0:T(2,128)(2,1)S(1)}, bf16[2,4096]{1,0:T(2,128)(2,1)}, u32[]{:S(2)}) copy-start(bf16[2,4096]{1,0:T(2,128)(2,1)} %refs_9_.1) | copy-start | bytes 49156
  13.5 6.1 %copy-start.1 = (bf16[2,4096]{1,0:T(2,128)(2,1)S(1)}, bf16[2,4096]{1,0:T(2,128)(2,1)}, u32[]{:S(2)}) copy-start(bf16[2,4096]{1,0:T(2,128)(2,1)} %refs_5_.3) | copy-start | bytes 49156

commit v6 on v5

--- a/solution.py
+++ b/solution.py
@@ -16,6 +16,7 @@
 F32, BF16 = jnp.float32, jnp.bfloat16
 CH = 128
 NB = 512
+LATE = 256
 LM = 39
 
 
@@ -165,16 +166,21 @@
     qkv_ref[...] = recvA[...]
 
 
-def _cache_copies(l, kc, vc, kb, vb, sem):
-    return [pltpu.make_async_copy(src.at[l, b], dst.at[b], sem.at[i, b])
-            for i, (src, dst) in enumerate(((kc, kb), (vc, vb))) for b in range(kb.shape[0])]
+def _cache_copies(l, kc, vc, kb, vb, sem, late=0):
+    nb, npos = kb.shape[:2]
+    out = []
+    for i, (src, dst) in enumerate(((kc, kb), (vc, vb))):
+        for b in range(nb):
+            n = npos - (late if i == 1 and b == nb - 1 else 0)
+            out.append(pltpu.make_async_copy(src.at[l, b, pl.ds(0, n)], dst.at[b, pl.ds(0, n)], sem.at[i, b]))
+    return out
 
 
 def _first(x, wq, wk, wv, g1h, kc, vc, h_ref, qkv_ref, kb, vb,
            wbuf, xm, xo, g1, sendA, recvA, wsem, xs, xr, sa, ra, gs, ks):
     dp, sp, c, me = _ids()
     cq = _qkv_copies(0, me, (wq, wk, wv), wbuf, wsem, 0, 0)
-    ck = _cache_copies(0, kc, vc, kb, vb, ks)
+    ck = _cache_copies(0, kc, vc, kb, vb, ks, LATE)
     _hello(me)
     cs = [pltpu.make_async_copy(x, xm, gs.at[0]), pltpu.make_async_copy(g1h, g1, gs.at[1])]
     for cp in cs + cq[:1]:
@@ -285,14 +291,18 @@
 
 def _attn(l, *refs):
     if l == 0:
-        lensh, qkv, kin, vin, ko, vo, op_ref, kb, vb, *sc = refs
+        lensh, qkv, kin, vin, vc, ko, vo, op_ref, kb, vb, *sc = refs
     else:
         lensh, qkv, kin, vin, _, _, ko, vo, op_ref, kb, vb, *sc = refs
-    tr, q_ref, s_ref, m_ref, l_ref, o_ref, kos, vos = sc
+    tr, q_ref, s_ref, m_ref, l_ref, o_ref, kos, vos, ls = sc
     nb, npos, nh, dh = kb.shape
     per = npos // CH
     n = nb * per
     base = lax.axis_index('sp') * npos
+    nlast = npos - LATE
+    if l == 0:
+        late = pltpu.make_async_copy(vc.at[l, nb - 1, pl.ds(nlast, LATE)], vb.at[nb - 1, pl.ds(nlast, LATE)], ls)
+        late.start()
     lv = lensh[...]
     lens = [jnp.max(lv[:, b:b + 1]) for b in range(nb)]
 
@@ -307,19 +317,22 @@
     m_ref[...] = jnp.full(m_ref.shape, -jnp.inf, F32)
     l_ref[...] = jnp.zeros_like(l_ref)
     o_ref[...] = jnp.zeros_like(o_ref)
+    def patch(buf, row, b):
+        lp = lens[b] - 1 - base
+
+        @pl.when((lp >= 0) & (lp < npos))
+        def _():
+            buf[b, lp] = tr[:, row + b, :].astype(BF16)
+
+    for b in range(nb):
+        patch(kb, 2, b)
+    for b in range(nb - 1):
+        patch(vb, 4, b)
     z = jnp.zeros((nh, dh), BF16)
     for b in range(nb):
         q = tr[:, b, :].astype(BF16)
         q_ref[b, 0:nh] = jnp.concatenate([q, z], axis=1)
         q_ref[b, nh:2 * nh] = jnp.concatenate([z, q], axis=1)
-    for b in range(nb):
-        lp = lens[b] - 1 - base
-
-        @pl.when((lp >= 0) & (lp < npos))
-        def _():
-            kb[b, lp] = tr[:, 2 + b, :].astype(BF16)
-            vb[b, lp] = tr[:, 4 + b, :].astype(BF16)
-
     hc = CH * nh // 2
     sl = lax.broadcasted_iota(jnp.int32, (8, dh), 0)
     ln = lax.broadcasted_iota(jnp.int32, (8, dh), 1)
@@ -347,6 +360,7 @@
 
     for i in range(n):
         wr(ko, kb, kos, i).start()
+    for i in range(n - per):
         wr(vo, vb, vos, i).start()
 
     def pick(b):
@@ -385,12 +399,17 @@
         return 0
 
     lax.fori_loop(0, nb, kstep, 0)
+    if l == 0:
+        late.wait()
+    patch(vb, 4, nb - 1)
+    mc = [column(m_ref[b], -jnp.inf, jnp.max) * sc for b in range(nb)]
+    for i in range(n - per, n):
+        wr(vo, vb, vos, i).start()
     lax.fori_loop(0, nb, vstep, 0)
     lane = lax.broadcasted_iota(jnp.int32, (nh, dh), 1)
     for b in range(nb):
         ov = o_ref[b, 0:nh, 0:dh] + o_ref[b, nh:2 * nh, dh:2 * dh]
-        mc = column(m_ref[b], -jnp.inf, jnp.max) * sc
-        ml = jnp.where(lane < 64, mc, column(l_ref[b], 0.0, jnp.sum))
+        ml = jnp.where(lane < 64, mc[b], column(l_ref[b], 0.0, jnp.sum))
         for r in range(8):
             op_ref[r, 0, b * 4:b * 4 + 4, :] = ov[4 * r:4 * r + 4]
             op_ref[r, 1, b * 4:b * 4 + 4, :] = ml[4 * r:4 * r + 4]
@@ -425,19 +444,19 @@
         def attn(l, qkv, kb, vb, ko, vo):
             n = nb * npos // CH
             c_sh = jax.ShapeDtypeStruct(kc.shape, kc.dtype)
-            args = vm(lens.reshape(1, nb), qkv, kb, vb) + ([] if l == 0 else hbm(ko, vo))
+            args = vm(lens.reshape(1, nb), qkv, kb, vb) + (hbm(vc) if l == 0 else hbm(ko, vo))
             al = {2: 3, 3: 4}
             if l > 0:
                 al.update({4: 0, 5: 1})
             return pl.pallas_call(
                 functools.partial(_attn, l),
                 out_shape=(c_sh, c_sh, V((8, 2, 8, dh), F32), c_vm, c_vm),
-                in_specs=[VM, VM, VM, VM] + ([] if l == 0 else [ANY, ANY]),
+                in_specs=[VM, VM, VM, VM] + ([ANY] if l == 0 else [ANY, ANY]),
                 out_specs=(ANY, ANY, VM, VM, VM),
                 scratch_shapes=[V((nh, 8, dh), F32), V((nb, 2 * nh, 2 * dh), BF16),
                                 V((n, 2, 8, CH * nh // 2), F32), V((nb, 8, dh), F32),
                                 V((nb, 8, dh), F32), V((nb, 2 * nh, 2 * dh), F32),
-                                DMA((n,)), DMA((n,))],
+                                DMA((n,)), DMA((n,)), DMA],
                 input_output_aliases=al,
                 compiler_params=pltpu.CompilerParams(vmem_limit_bytes=14 * 2 ** 20), name='attn')(*args)[:3]
 

time: 74.4 us -> 73.6 us (0.989)
  Pallas kernels: 72.9 us -> 72.1 us
where the time goes in v6:
time: 73.6 us; the launch traced here: 73.5 us
  Pallas kernels  72.1 us (98%)
    pallas_call x2, Pallas kernels, layer(): pl.pallas_call(functools.partial(_layer, l, last), out_shape=outs, in_spe...  47.6 us
    pallas_call x1, Pallas kernels, local(): pl.pallas_call(_first, out_shape=(h_sh, qkv_sh, c_vm, c_vm), in_specs=[AN...  12.4 us
    pallas_call x2, Pallas kernels, attn(): pl.pallas_call(functools.partial(_attn, l), out_shape=(c_sh, c_sh, V((8,...  12.2 us

profile of v6, /device:TPU:0, one launch (start us, length us, event | category | flops | bytes accessed | tf_op | source)
XLA Modules:
  0.0 73.5 jit_solution(16065909561887647371)
XLA Ops:
  0.6 0.0 copy-start.2
  0.6 12.4 %first.1 = (f32[8,4096]{1,0:T(8,128)S(1)}, bf16[8,8,512]{2,1,0:T(8,128)(2,1)S(1)}, bf16[2,512,32,128]{3,2,1,0:T(8,128)(2,1)S(1)}, bf16[2,512,32,128]{3,2,1,0:T(8,128)(2,1)S(1)}) custom-call(bf16[2,4096]{1,0:T(2,128)(2,1)} %x.1, bf16[2,4096,4096]{2,1,0:T(8,128)(2,1)} %refs_6_.1, bf16[2,4096,4096]{2,1,0:T(8,128)(2,1)} %refs_7_.1, ...), custom_call_target="tpu_custom_call" | custom-call | tf_op jit(solution)/shard_map/first/pallas_call | solution.py:437
  13.0 0.0 copy-done.2
  13.0 0.0 copy-start
  13.1 0.0 copy-start.1
  13.1 6.1 %attn.2 = (bf16[2,2,512,32,128]{4,3,2,1,0:T(8,128)(2,1)}, bf16[2,2,512,32,128]{4,3,2,1,0:T(8,128)(2,1)}, f32[8,2,8,128]{3,2,1,0:T(8,128)S(1)}, bf16[2,512,32,128...) custom-call(s32[1,2]{1,0:T(1,128)S(1)} %bitcast.1, ...), custom_call_target="tpu_custom_call", output_to_operand_aliasing={{3}: (2, {}), {4}: (3, {})} | custom-call | tf_op jit(solution)/shard_map/attn/pallas_call | solution.py:451
  19.2 0.0 copy-done
  19.2 0.0 copy-done.1
  19.2 26.9 %layer.2 = (f32[8,4096]{1,0:T(8,128)S(1)}, bf16[8,8,512]{2,1,0:T(8,128)(2,1)S(1)}, bf16[2,512,32,128]{3,2,1,0:T(8,128)(2,1)S(1)}, bf16[2,512,32,128]{3,2,1,0:T(8,128)(2,1)S(1)}) custom-call(f32[8,2,8,128]{3,2,1,0:T(8,128)S(1)} %get-tuple-element.20.refs_0_, f32[8,4096]{1,0:T(8,128)S(1)} %get-tuple-element.21.refs_1_, bf16[2,1024,4096]{2,1,0:T(8,128)(2,1)} %refs_2_.3, ...), custom_call_target="tpu_custom_call" | custom-call | tf_op jit(solution)/shard_map/layer/pallas_call | solution.py:480
  46.1 6.1 %attn.3 = (bf16[2,2,512,32,128]{4,3,2,1,0:T(8,128)(2,1)}, bf16[2,2,512,32,128]{4,3,2,1,0:T(8,128)(2,1)}, f32[8,2,8,128]{3,2,1,0:T(8,128)S(1)}, bf16[2,512,32,128...) custom-call(s32[1,2]{1,0:T(1,128)S(1)} %bitcast.2, ...), custom_call_target="tpu_custom_call", output_to_operand_aliasing={{3}: (2, {}), {4}: (3, {}), {0}: (4, {}), {1}: (5, {})} | custom-call | tf_op jit(solution)/shard_map/attn/pallas_call | solution.py:451
  52.1 20.7 %layer.3 = bf16[2,4096]{1,0:T(2,128)(2,1)S(1)} custom-call(f32[8,2,8,128]{3,2,1,0:T(8,128)S(1)} %get-tuple-element.27.refs_0_, f32[8,4096]{1,0:T(8,128)S(1)} %get-tuple-element.28.refs_1_, bf16[2,1024,4096]{2,1,0:T(8,128)(2,1)} %refs_2_.3, bf16[2,4096,4096]{2,1,0:T(8,128)(2,1)} %refs_3_.3, bf16[2,4096,4096]{2,1,0:T(8,128)(2,1)} %refs_4_.5, ...), custom_call_target="tpu_custom_call" | custom-call | tf_op jit(solution)/shard_map/layer/pallas_call | solution.py:480
  72.9 0.6 copy.28
Async XLA Ops:
  0.6 12.4 %copy-start.2 = (s32[2]{0:T(128)S(1)}, s32[2]{0:T(128)}, u32[]{:S(2)}) copy-start(s32[2]{0:T(128)} %param.13) | copy-start | bytes 28
  13.0 6.1 %copy-start = (bf16[2,4096]{1,0:T(2,128)(2,1)S(1)}, bf16[2,4096]{1,0:T(2,128)(2,1)}, u32[]{:S(2)}) copy-start(bf16[2,4096]{1,0:T(2,128)(2,1)} %refs_9_.1) | copy-start | bytes 49156
  13.1 6.1 %copy-start.1 = (bf16[2,4096]{1,0:T(2,128)(2,1)S(1)}, bf16[2,4096]{1,0:T(2,128)(2,1)}, u32[]{:S(2)}) copy-start(bf16[2,4096]{1,0:T(2,128)(2,1)} %refs_5_.3) | copy-start | bytes 49156

commit v7 on v6

--- a/solution.py
+++ b/solution.py
@@ -14,7 +14,7 @@
 ANY = pl.BlockSpec(memory_space=pltpu.HBM)
 SM = pl.BlockSpec(memory_space=pltpu.SMEM)
 F32, BF16 = jnp.float32, jnp.bfloat16
-CH = 128
+CH = 256
 NB = 512
 LATE = 256
 LM = 39
@@ -310,6 +310,21 @@
         b, p = i // per, pl.multiple_of(lax.rem(i, per) * CH, CH)
         return pltpu.make_async_copy(buf.at[b, pl.ds(p, CH)], dst.at[l, b, pl.ds(p, CH)], sem.at[i])
 
+    own = [lens[b] - 1 - base for b in range(nb)]
+    first_v = [(vo, vb, vos, i, 4) for i in range(n if l > 0 else n - per)]
+    early = [(ko, kb, kos, i, 2) for i in range(n)] + first_v
+    last_v = [(vo, vb, vos, i, 4) for i in range(len(first_v), n)]
+
+    def send(jobs, patched):
+        for dst, buf, sem, i, _ in jobs:
+            p0 = i % per * CH
+            here = (own[i // per] >= p0) & (own[i // per] < p0 + CH)
+
+            @pl.when(here if patched else jnp.logical_not(here))
+            def _():
+                wr(dst, buf, sem, i).start()
+
+    send(early, False)
     for src in range(8):
         v = qkv[src].astype(F32)
         for j in range(4):
@@ -317,8 +332,9 @@
     m_ref[...] = jnp.full(m_ref.shape, -jnp.inf, F32)
     l_ref[...] = jnp.zeros_like(l_ref)
     o_ref[...] = jnp.zeros_like(o_ref)
+
     def patch(buf, row, b):
-        lp = lens[b] - 1 - base
+        lp = own[b]
 
         @pl.when((lp >= 0) & (lp < npos))
         def _():
@@ -326,7 +342,7 @@
 
     for b in range(nb):
         patch(kb, 2, b)
-    for b in range(nb - 1):
+    for b in range(nb if l > 0 else nb - 1):
         patch(vb, 4, b)
     z = jnp.zeros((nh, dh), BF16)
     for b in range(nb):
@@ -358,10 +374,7 @@
         return jnp.concatenate([buf[b, pl.ds(p0, CH // 2)].reshape(hc, dh),
                                 buf[b, pl.ds(p0 + CH // 2, CH // 2)].reshape(hc, dh)], axis=1)
 
-    for i in range(n):
-        wr(ko, kb, kos, i).start()
-    for i in range(n - per):
-        wr(vo, vb, vos, i).start()
+    send(early, True)
 
     def pick(b):
         return functools.reduce(lambda v, i: jnp.where(b == i, lens[i], v), range(1, nb), lens[0])
@@ -401,10 +414,10 @@
     lax.fori_loop(0, nb, kstep, 0)
     if l == 0:
         late.wait()
-    patch(vb, 4, nb - 1)
+        send(last_v, False)
+        patch(vb, 4, nb - 1)
     mc = [column(m_ref[b], -jnp.inf, jnp.max) * sc for b in range(nb)]
-    for i in range(n - per, n):
-        wr(vo, vb, vos, i).start()
+    send(last_v, True)
     lax.fori_loop(0, nb, vstep, 0)
     lane = lax.broadcasted_iota(jnp.int32, (nh, dh), 1)
     for b in range(nb):

time: 73.6 us -> 73.4 us (level)
  no operation moved by 1% of the time
where the time goes in v7:
time: 73.4 us; the launch traced here: 73.3 us
  Pallas kernels  72 us (98%)
    pallas_call x2, Pallas kernels, layer(): pl.pallas_call(functools.partial(_layer, l, last), out_shape=outs, in_spe...  47.6 us
    pallas_call x1, Pallas kernels, local(): pl.pallas_call(_first, out_shape=(h_sh, qkv_sh, c_vm, c_vm), in_specs=[AN...  12.4 us
    pallas_call x2, Pallas kernels, attn(): pl.pallas_call(functools.partial(_attn, l), out_shape=(c_sh, c_sh, V((8,...  12 us

profile of v7, /device:TPU:0, one launch (start us, length us, event | category | flops | bytes accessed | tf_op | source)
XLA Modules:
  0.0 73.3 jit_solution(12826610205667091725)
XLA Ops:
  0.6 0.0 copy-start.2
  0.6 12.4 %first.1 = (f32[8,4096]{1,0:T(8,128)S(1)}, bf16[8,8,512]{2,1,0:T(8,128)(2,1)S(1)}, bf16[2,512,32,128]{3,2,1,0:T(8,128)(2,1)S(1)}, bf16[2,512,32,128]{3,2,1,0:T(8,128)(2,1)S(1)}) custom-call(bf16[2,4096]{1,0:T(2,128)(2,1)} %x.1, bf16[2,4096,4096]{2,1,0:T(8,128)(2,1)} %refs_6_.1, bf16[2,4096,4096]{2,1,0:T(8,128)(2,1)} %refs_7_.1, ...), custom_call_target="tpu_custom_call" | custom-call | tf_op jit(solution)/shard_map/first/pallas_call | solution.py:450
  13.0 0.0 copy-done.2
  13.0 0.0 copy-start
  13.1 0.0 copy-start.1
  13.1 6.0 %attn.2 = (bf16[2,2,512,32,128]{4,3,2,1,0:T(8,128)(2,1)}, bf16[2,2,512,32,128]{4,3,2,1,0:T(8,128)(2,1)}, f32[8,2,8,128]{3,2,1,0:T(8,128)S(1)}, bf16[2,512,32,128...) custom-call(s32[1,2]{1,0:T(1,128)S(1)} %bitcast.1, ...), custom_call_target="tpu_custom_call", output_to_operand_aliasing={{3}: (2, {}), {4}: (3, {})} | custom-call | tf_op jit(solution)/shard_map/attn/pallas_call | solution.py:464
  19.1 0.0 copy-done
  19.1 0.0 copy-done.1
  19.1 26.9 %layer.2 = (f32[8,4096]{1,0:T(8,128)S(1)}, bf16[8,8,512]{2,1,0:T(8,128)(2,1)S(1)}, bf16[2,512,32,128]{3,2,1,0:T(8,128)(2,1)S(1)}, bf16[2,512,32,128]{3,2,1,0:T(8,128)(2,1)S(1)}) custom-call(f32[8,2,8,128]{3,2,1,0:T(8,128)S(1)} %get-tuple-element.20.refs_0_, f32[8,4096]{1,0:T(8,128)S(1)} %get-tuple-element.21.refs_1_, bf16[2,1024,4096]{2,1,0:T(8,128)(2,1)} %refs_2_.3, ...), custom_call_target="tpu_custom_call" | custom-call | tf_op jit(solution)/shard_map/layer/pallas_call | solution.py:493
  46.0 6.0 %attn.3 = (bf16[2,2,512,32,128]{4,3,2,1,0:T(8,128)(2,1)}, bf16[2,2,512,32,128]{4,3,2,1,0:T(8,128)(2,1)}, f32[8,2,8,128]{3,2,1,0:T(8,128)S(1)}, bf16[2,512,32,128...) custom-call(s32[1,2]{1,0:T(1,128)S(1)} %bitcast.2, ...), custom_call_target="tpu_custom_call", output_to_operand_aliasing={{3}: (2, {}), {4}: (3, {}), {0}: (4, {}), {1}: (5, {})} | custom-call | tf_op jit(solution)/shard_map/attn/pallas_call | solution.py:464
  52.0 20.7 %layer.3 = bf16[2,4096]{1,0:T(2,128)(2,1)S(1)} custom-call(f32[8,2,8,128]{3,2,1,0:T(8,128)S(1)} %get-tuple-element.27.refs_0_, f32[8,4096]{1,0:T(8,128)S(1)} %get-tuple-element.28.refs_1_, bf16[2,1024,4096]{2,1,0:T(8,128)(2,1)} %refs_2_.3, bf16[2,4096,4096]{2,1,0:T(8,128)(2,1)} %refs_3_.3, bf16[2,4096,4096]{2,1,0:T(8,128)(2,1)} %refs_4_.5, ...), custom_call_target="tpu_custom_call" | custom-call | tf_op jit(solution)/shard_map/layer/pallas_call | solution.py:493
  72.7 0.6 copy.28
Async XLA Ops:
  0.6 12.4 %copy-start.2 = (s32[2]{0:T(128)S(1)}, s32[2]{0:T(128)}, u32[]{:S(2)}) copy-start(s32[2]{0:T(128)} %param.13) | copy-start | bytes 28
  13.0 6.0 %copy-start = (bf16[2,4096]{1,0:T(2,128)(2,1)S(1)}, bf16[2,4096]{1,0:T(2,128)(2,1)}, u32[]{:S(2)}) copy-start(bf16[2,4096]{1,0:T(2,128)(2,1)} %refs_9_.1) | copy-start | bytes 49156
  13.1 6.0 %copy-start.1 = (bf16[2,4096]{1,0:T(2,128)(2,1)S(1)}, bf16[2,4096]{1,0:T(2,128)(2,1)}, u32[]{:S(2)}) copy-start(bf16[2,4096]{1,0:T(2,128)(2,1)} %refs_5_.3) | copy-start | bytes 49156

commit v8 on v7

--- a/solution.py
+++ b/solution.py
@@ -102,7 +102,7 @@
     return out
 
 
-def _allreduce(block, dp, sp, c, buf, sems, h_ref):
+def _allreduce(block, dp, sp, c, buf, sems, h_ref, more=()):
     psend, pown, precv, chips, tot = buf
     s1, r1, s2, r2, s3, r3 = sems
     x = sp // 2
@@ -129,6 +129,8 @@
         chips[chip, t] = pown[t] + precv[t]
         for cp in two[t]:
             cp.start()
+    for cp in more:
+        cp.start()
     for t in range(2):
         for cp in two[t]:
             cp.wait()
@@ -259,8 +261,6 @@
         return [s1.at[i], r1.at[i], s2.at[i], r2.at[i], s3.at[i], r3.at[i]]
 
     _allreduce(wo_block, dp, sp, c, bufs(0), sems(0), h_ref)
-    for cp in ck:
-        cp.start()
     xn = _rms(h_ref[...], g2[l:l + 1, :])
     for cp in cm[8:16]:
         cp.wait()
@@ -271,7 +271,7 @@
     uv = u[...]
     for cp in cm[16:]:
         cp.wait()
-    for cp in cq:
+    for cp in cq + ck:
         cp.start()
 
     def w2_block(t, q):

time: 73.4 us -> 72.5 us (0.988)
  Pallas kernels: 72 us -> 71.1 us
    pallas_call x2, Pallas kernels: 47.6 us -> 46.7 us  [layer(): pl.pallas_call(functools.partial(_layer, l, last), out_shape=outs, in_spe...]
where the time goes in v8:
time: 72.5 us; the launch traced here: 72.4 us
  Pallas kernels  71.1 us (98%)
    pallas_call x2, Pallas kernels, layer(): pl.pallas_call(functools.partial(_layer, l, last), out_shape=outs, in_spe...  46.7 us
    pallas_call x1, Pallas kernels, local(): pl.pallas_call(_first, out_shape=(h_sh, qkv_sh, c_vm, c_vm), in_specs=[AN...  12.4 us
    pallas_call x2, Pallas kernels, attn(): pl.pallas_call(functools.partial(_attn, l), out_shape=(c_sh, c_sh, V((8,...  12 us

profile of v8, /device:TPU:0, one launch (start us, length us, event | category | flops | bytes accessed | tf_op | source)
XLA Modules:
  0.0 72.4 jit_solution(5083749721710898777)
XLA Ops:
  0.6 0.0 copy-start.2
  0.6 12.4 %first.1 = (f32[8,4096]{1,0:T(8,128)S(1)}, bf16[8,8,512]{2,1,0:T(8,128)(2,1)S(1)}, bf16[2,512,32,128]{3,2,1,0:T(8,128)(2,1)S(1)}, bf16[2,512,32,128]{3,2,1,0:T(8,128)(2,1)S(1)}) custom-call(bf16[2,4096]{1,0:T(2,128)(2,1)} %x.1, bf16[2,4096,4096]{2,1,0:T(8,128)(2,1)} %refs_6_.1, bf16[2,4096,4096]{2,1,0:T(8,128)(2,1)} %refs_7_.1, ...), custom_call_target="tpu_custom_call" | custom-call | tf_op jit(solution)/shard_map/first/pallas_call | solution.py:450
  13.0 0.0 copy-done.2
  13.0 0.0 copy-start
  13.1 0.0 copy-start.1
  13.1 6.0 %attn.2 = (bf16[2,2,512,32,128]{4,3,2,1,0:T(8,128)(2,1)}, bf16[2,2,512,32,128]{4,3,2,1,0:T(8,128)(2,1)}, f32[8,2,8,128]{3,2,1,0:T(8,128)S(1)}, bf16[2,512,32,128...) custom-call(s32[1,2]{1,0:T(1,128)S(1)} %bitcast.1, ...), custom_call_target="tpu_custom_call", output_to_operand_aliasing={{3}: (2, {}), {4}: (3, {})} | custom-call | tf_op jit(solution)/shard_map/attn/pallas_call | solution.py:464
  19.1 0.0 copy-done
  19.1 0.0 copy-done.1
  19.1 26.0 %layer.2 = (f32[8,4096]{1,0:T(8,128)S(1)}, bf16[8,8,512]{2,1,0:T(8,128)(2,1)S(1)}, bf16[2,512,32,128]{3,2,1,0:T(8,128)(2,1)S(1)}, bf16[2,512,32,128]{3,2,1,0:T(8,128)(2,1)S(1)}) custom-call(f32[8,2,8,128]{3,2,1,0:T(8,128)S(1)} %get-tuple-element.20.refs_0_, f32[8,4096]{1,0:T(8,128)S(1)} %get-tuple-element.21.refs_1_, bf16[2,1024,4096]{2,1,0:T(8,128)(2,1)} %refs_2_.3, ...), custom_call_target="tpu_custom_call" | custom-call | tf_op jit(solution)/shard_map/layer/pallas_call | solution.py:493
  45.1 6.0 %attn.3 = (bf16[2,2,512,32,128]{4,3,2,1,0:T(8,128)(2,1)}, bf16[2,2,512,32,128]{4,3,2,1,0:T(8,128)(2,1)}, f32[8,2,8,128]{3,2,1,0:T(8,128)S(1)}, bf16[2,512,32,128...) custom-call(s32[1,2]{1,0:T(1,128)S(1)} %bitcast.2, ...), custom_call_target="tpu_custom_call", output_to_operand_aliasing={{3}: (2, {}), {4}: (3, {}), {0}: (4, {}), {1}: (5, {})} | custom-call | tf_op jit(solution)/shard_map/attn/pallas_call | solution.py:464
  51.1 20.7 %layer.3 = bf16[2,4096]{1,0:T(2,128)(2,1)S(1)} custom-call(f32[8,2,8,128]{3,2,1,0:T(8,128)S(1)} %get-tuple-element.27.refs_0_, f32[8,4096]{1,0:T(8,128)S(1)} %get-tuple-element.28.refs_1_, bf16[2,1024,4096]{2,1,0:T(8,128)(2,1)} %refs_2_.3, bf16[2,4096,4096]{2,1,0:T(8,128)(2,1)} %refs_3_.3, bf16[2,4096,4096]{2,1,0:T(8,128)(2,1)} %refs_4_.5, ...), custom_call_target="tpu_custom_call" | custom-call | tf_op jit(solution)/shard_map/layer/pallas_call | solution.py:493
  71.8 0.6 copy.28
Async XLA Ops:
  0.6 12.4 %copy-start.2 = (s32[2]{0:T(128)S(1)}, s32[2]{0:T(128)}, u32[]{:S(2)}) copy-start(s32[2]{0:T(128)} %param.13) | copy-start | bytes 28
  13.0 6.1 %copy-start = (bf16[2,4096]{1,0:T(2,128)(2,1)S(1)}, bf16[2,4096]{1,0:T(2,128)(2,1)}, u32[]{:S(2)}) copy-start(bf16[2,4096]{1,0:T(2,128)(2,1)} %refs_9_.1) | copy-start | bytes 49156
  13.1 6.0 %copy-start.1 = (bf16[2,4096]{1,0:T(2,128)(2,1)S(1)}, bf16[2,4096]{1,0:T(2,128)(2,1)}, u32[]{:S(2)}) copy-start(bf16[2,4096]{1,0:T(2,128)(2,1)} %refs_5_.3) | copy-start | bytes 49156

commit v9 on v8

--- a/solution.py
+++ b/solution.py
@@ -124,9 +124,9 @@
         psend[t] = both(t)
         one[t].start()
     for t in range(2):
-        pown[t] = both(2 + t)
+        mine = both(2 + t)
         one[t].wait()
-        chips[chip, t] = pown[t] + precv[t]
+        chips[chip, t] = mine + precv[t]
         for cp in two[t]:
             cp.start()
     for cp in more:

time: 72.5 us -> 72.5 us (level)
  no operation moved by 1% of the time
where the time goes in v9:
time: 72.5 us; the launch traced here: 72.4 us
  Pallas kernels  71.1 us (98%)
    pallas_call x2, Pallas kernels, layer(): pl.pallas_call(functools.partial(_layer, l, last), out_shape=outs, in_spe...  46.7 us
    pallas_call x1, Pallas kernels, local(): pl.pallas_call(_first, out_shape=(h_sh, qkv_sh, c_vm, c_vm), in_specs=[AN...  12.4 us
    pallas_call x2, Pallas kernels, attn(): pl.pallas_call(functools.partial(_attn, l), out_shape=(c_sh, c_sh, V((8,...  12 us

profile of v9, /device:TPU:0, one launch (start us, length us, event | category | flops | bytes accessed | tf_op | source)
XLA Modules:
  0.0 72.4 jit_solution(5083749721710898777)
XLA Ops:
  0.6 0.0 copy-start.2
  0.6 12.4 %first.1 = (f32[8,4096]{1,0:T(8,128)S(1)}, bf16[8,8,512]{2,1,0:T(8,128)(2,1)S(1)}, bf16[2,512,32,128]{3,2,1,0:T(8,128)(2,1)S(1)}, bf16[2,512,32,128]{3,2,1,0:T(8,128)(2,1)S(1)}) custom-call(bf16[2,4096]{1,0:T(2,128)(2,1)} %x.1, bf16[2,4096,4096]{2,1,0:T(8,128)(2,1)} %refs_6_.1, bf16[2,4096,4096]{2,1,0:T(8,128)(2,1)} %refs_7_.1, ...), custom_call_target="tpu_custom_call" | custom-call | tf_op jit(solution)/shard_map/first/pallas_call | solution.py:450
  13.0 0.0 copy-done.2
  13.0 0.0 copy-start
  13.1 0.0 copy-start.1
  13.1 6.0 %attn.2 = (bf16[2,2,512,32,128]{4,3,2,1,0:T(8,128)(2,1)}, bf16[2,2,512,32,128]{4,3,2,1,0:T(8,128)(2,1)}, f32[8,2,8,128]{3,2,1,0:T(8,128)S(1)}, bf16[2,512,32,128...) custom-call(s32[1,2]{1,0:T(1,128)S(1)} %bitcast.1, ...), custom_call_target="tpu_custom_call", output_to_operand_aliasing={{3}: (2, {}), {4}: (3, {})} | custom-call | tf_op jit(solution)/shard_map/attn/pallas_call | solution.py:464
  19.1 0.0 copy-done
  19.1 0.0 copy-done.1
  19.1 26.0 %layer.2 = (f32[8,4096]{1,0:T(8,128)S(1)}, bf16[8,8,512]{2,1,0:T(8,128)(2,1)S(1)}, bf16[2,512,32,128]{3,2,1,0:T(8,128)(2,1)S(1)}, bf16[2,512,32,128]{3,2,1,0:T(8,128)(2,1)S(1)}) custom-call(f32[8,2,8,128]{3,2,1,0:T(8,128)S(1)} %get-tuple-element.20.refs_0_, f32[8,4096]{1,0:T(8,128)S(1)} %get-tuple-element.21.refs_1_, bf16[2,1024,4096]{2,1,0:T(8,128)(2,1)} %refs_2_.3, ...), custom_call_target="tpu_custom_call" | custom-call | tf_op jit(solution)/shard_map/layer/pallas_call | solution.py:493
  45.1 6.0 %attn.3 = (bf16[2,2,512,32,128]{4,3,2,1,0:T(8,128)(2,1)}, bf16[2,2,512,32,128]{4,3,2,1,0:T(8,128)(2,1)}, f32[8,2,8,128]{3,2,1,0:T(8,128)S(1)}, bf16[2,512,32,128...) custom-call(s32[1,2]{1,0:T(1,128)S(1)} %bitcast.2, ...), custom_call_target="tpu_custom_call", output_to_operand_aliasing={{3}: (2, {}), {4}: (3, {}), {0}: (4, {}), {1}: (5, {})} | custom-call | tf_op jit(solution)/shard_map/attn/pallas_call | solution.py:464
  51.1 20.7 %layer.3 = bf16[2,4096]{1,0:T(2,128)(2,1)S(1)} custom-call(f32[8,2,8,128]{3,2,1,0:T(8,128)S(1)} %get-tuple-element.27.refs_0_, f32[8,4096]{1,0:T(8,128)S(1)} %get-tuple-element.28.refs_1_, bf16[2,1024,4096]{2,1,0:T(8,128)(2,1)} %refs_2_.3, bf16[2,4096,4096]{2,1,0:T(8,128)(2,1)} %refs_3_.3, bf16[2,4096,4096]{2,1,0:T(8,128)(2,1)} %refs_4_.5, ...), custom_call_target="tpu_custom_call" | custom-call | tf_op jit(solution)/shard_map/layer/pallas_call | solution.py:493
  71.8 0.6 copy.28
Async XLA Ops:
  0.6 12.4 %copy-start.2 = (s32[2]{0:T(128)S(1)}, s32[2]{0:T(128)}, u32[]{:S(2)}) copy-start(s32[2]{0:T(128)} %param.13) | copy-start | bytes 28
  13.0 6.0 %copy-start = (bf16[2,4096]{1,0:T(2,128)(2,1)S(1)}, bf16[2,4096]{1,0:T(2,128)(2,1)}, u32[]{:S(2)}) copy-start(bf16[2,4096]{1,0:T(2,128)(2,1)} %refs_9_.1) | copy-start | bytes 49156
  13.1 6.0 %copy-start.1 = (bf16[2,4096]{1,0:T(2,128)(2,1)S(1)}, bf16[2,4096]{1,0:T(2,128)(2,1)}, u32[]{:S(2)}) copy-start(bf16[2,4096]{1,0:T(2,128)(2,1)} %refs_5_.3) | copy-start | bytes 49156
